TPU v7x, 32 devices: a whole 2x2x4 slice. The times are simulated.
32 devices in a mesh: cond: 2 (over x), gx: 4 (over y, core), yz: 4 (over z).
Axes of the slice: x: 2, y: 2, z: 4, core: 2. Of those that a mesh axis runs over, the one named last changes fastest.
Arguments:
- adjoint: float32 [2, 5, 32, 64, 256], P('cond', None, 'gx', 'yz'), may hold values from -6 to 6
- objective_gradient: float32 [2, 5, 32, 64, 256], P('cond', None, 'gx', 'yz'), may hold values from -6 to 6
- diagonal: float32 [32, 64, 256], P('gx', 'yz'), may hold values from 4 to 12
- flux_blocks: float32 [2, 6, 5, 5], P('cond'), may hold values from -1 to 1
- flux_sensitivity: bfloat16 [2, 5, 32, 64, 256], P('cond', None, 'gx', 'yz'), may hold values from -6 to 6
- surface_mask: int32 [32, 64, 256], P('gx', 'yz'), may hold values 0 or 1
- patch_band_slot: int32 [32, 64], P('gx', 'yz'), may hold values from 0 to 62
- design_basis: float32 [256, 128], replicated, may hold values from -0.046875 to 0.046875
- condition_weights: int32 [2], replicated, may hold values from 1 to 999, as said below
Outputs:
- smoothed: float32 [2, 5, 32, 64, 256], P('cond', None, 'gx', 'yz')
- residual: float32 [2, 5, 32, 64, 256], P('cond', None, 'gx', 'yz')
- design_gradient: float32 [4096], P(('gx', 'yz'))
Inputs may be any that keep to these rules, and one draw needn't show every extreme that they name: `condition_weights`: positive integer weights; one condition has weight 999.
All inputs are finite; a program needn't handle non-finite values. No bound on the sum of `surface_mask` on one device may be relied on, other than what follows from the above.
Results may differ from a plain program's by a relative error of at most 0.0003.
Values sent between devices are 32-bit elements; how exact they have to be, the bound alone decides.
A program may use at most 64 MiB of HBM per device.

v0:
```python
import functools

import jax
import jax.numpy as jnp
from jax import lax
from jax.experimental import pallas as pl
from jax.experimental.pallas import tpu as pltpu
from jax.sharding import PartitionSpec as P

NDES = 4096
RELAX = 0.8
LANES = 128
PAD = 8
MESH = pl.DeviceIdType.MESH


def kernel(
    sizes,
    adjoint,
    source_hbm,
    diagonal_hbm,
    flux,
    sensitivity_hbm,
    mask_hbm,
    slots_hbm,
    basis_hbm,
    weights,
    smoothed_out,
    residual_out,
    gradient_out,
    fields,
    source,
    diagonal,
    sensitivity,
    mask,
    slots,
    basis,
    surface,
    pieces,
    arrived,
    local_sems,
    plane_sems,
    first_sems,
    row_sems,
    face_sems,
    piece_sems,
):
    n_cond, n_gx, n_yz = sizes
    devices = n_cond * n_gx * n_yz
    nvar, nx, ny, nz = source.shape
    halves = nz // LANES
    rows = pieces.shape[1]
    per_owner = NDES // (n_gx * n_yz)
    ci, xi, yi = lax.axis_index("cond"), lax.axis_index("gx"), lax.axis_index("yz")
    me = (ci * n_gx + xi) * n_yz + yi

    def place(flat):
        return (flat // (n_gx * n_yz), (flat // n_yz) % n_gx, flat % n_yz)

    barrier = pltpu.get_barrier_semaphore()

    def for_others(action):
        if devices <= 64:
            here = (ci, xi, yi)
            turns = [[(p + t) % n for t in range(n)] for p, n in zip(here, sizes)]
            for dy in range(n_yz):
                for dx in range(n_gx):
                    for dc in range(n_cond):
                        if dc or dx or dy:
                            action(turns[0][dc], turns[1][dx], turns[2][dy])
        else:

            def step(t, carry):
                action(*place((me + t) % devices))
                return carry

            lax.fori_loop(1, devices, step, 0)

    def greet(c, gx, yz):
        pl.semaphore_signal(barrier, inc=1, device_id=(c, gx, yz), device_id_type=MESH)

    for_others(greet)
    inner_y = pl.ds(PAD, ny)

    def plane_loads(x):
        pairs = [
            (
                adjoint.at[0, :, x, :, pl.ds(h * LANES, LANES)],
                fields.at[0, :, x + 1, h, inner_y, :],
            )
            for h in range(halves)
        ]
        pairs.append((source_hbm.at[0, :, x], source.at[:, x]))
        pairs.append((diagonal_hbm.at[x], diagonal.at[x]))
        return [
            pltpu.make_async_copy(src, dst, plane_sems.at[i, x])
            for i, (src, dst) in enumerate(pairs)
        ]

    late_loads = [
        pltpu.make_async_copy(src, dst, local_sems.at[i])
        for i, (src, dst) in enumerate(
            (
                (sensitivity_hbm.at[0], sensitivity),
                (mask_hbm, mask),
                (slots_hbm, slots),
                (basis_hbm, basis),
            )
        )
    ]
    for x in range(nx):
        for copy in plane_loads(x):
            copy.start()
    for copy in late_loads:
        copy.start()

    has_before_x, has_after_x = xi > 0, xi < n_gx - 1
    has_before_y, has_after_y = yi > 0, yi < n_yz - 1

    blank_x = jnp.zeros((nvar, halves, ny, LANES), jnp.float32)
    blank_y = jnp.zeros((nvar, nx, halves, 1, LANES), jnp.float32)

    def clear_x(stage, x):
        fields[stage, :, x, :, PAD : PAD + ny, :] = blank_x

    def clear_y(stage, y):
        fields[stage, :, 1 : nx + 1, :, y : y + 1, :] = blank_y

    for stage in range(3):
        pl.when(xi == 0)(functools.partial(clear_x, stage, 0))
        pl.when(xi == n_gx - 1)(functools.partial(clear_x, stage, nx + 1))
        pl.when(yi == 0)(functools.partial(clear_y, stage, PAD - 1))
        pl.when(yi == n_yz - 1)(functools.partial(clear_y, stage, PAD + ny))

    def remote(src, dst, sems, target):
        return pltpu.make_async_remote_copy(
            src_ref=src,
            dst_ref=dst,
            send_sem=sems[0],
            recv_sem=sems[1],
            device_id=target,
            device_id_type=MESH,
        )

    after_x, before_x = (ci, xi + 1, yi), (ci, xi - 1, yi)
    after_y, before_y = (ci, xi, yi + 1), (ci, xi, yi - 1)

    first_y, first_x = [], []
    for h in range(halves):
        lanes = pl.ds(h * LANES, LANES)

        def sems(way, h=h):
            return first_sems.at[0, way, h], first_sems.at[1, way, h]

        inner_x = pl.ds(1, nx)
        first_y.append((has_after_y, has_before_y, remote(
            adjoint.at[0, :, :, pl.ds(ny - 1, 1), lanes],
            fields.at[0, :, inner_x, h, pl.ds(PAD - 1, 1), :], sems(0), after_y)))
        first_y.append((has_before_y, has_after_y, remote(
            adjoint.at[0, :, :, pl.ds(0, 1), lanes],
            fields.at[0, :, inner_x, h, pl.ds(PAD + ny, 1), :], sems(1), before_y)))
        first_x.append((has_after_x, has_before_x, remote(
            adjoint.at[0, :, nx - 1, :, lanes],
            fields.at[0, :, 0, h, inner_y, :], sems(2), after_x)))
        first_x.append((has_before_x, has_after_x, remote(
            adjoint.at[0, :, 0, :, lanes],
            fields.at[0, :, nx + 1, h, inner_y, :], sems(3), before_x)))

    def row_copies(stage, x):
        def sems(way):
            return row_sems.at[stage - 1, 0, way, x], row_sems.at[stage - 1, 1, way, x]

        def row(y):
            return fields.at[stage, :, x + 1, :, pl.ds(y, 1), :]

        return [
            (has_after_y, has_before_y, remote(row(PAD + ny - 1), row(PAD - 1), sems(0), after_y)),
            (has_before_y, has_after_y, remote(row(PAD), row(PAD + ny), sems(1), before_y)),
        ]

    def face_copies(stage):
        def sems(way):
            return face_sems.at[stage - 1, 0, way], face_sems.at[stage - 1, 1, way]

        def face(x):
            return fields.at[stage, :, x, :, inner_y, :]

        return [
            (has_after_x, has_before_x, remote(face(nx), face(0), sems(0), after_x)),
            (has_before_x, has_after_x, remote(face(1), face(nx + 1), sems(1), before_x)),
        ]

    def begin(plans):
        for go, _, copy in plans:
            pl.when(go)(copy.start)

    def receive(plans):
        for _, come, copy in plans:
            pl.when(come)(copy.wait_recv)

    def drain(plans):
        for go, _, copy in plans:
            pl.when(go)(copy.wait_send)

    pl.semaphore_wait(barrier, devices - 1)
    begin(first_y)
    begin(first_x)

    def plane_of(step):
        return jnp.where(step < nx - 2, step + 1, jnp.where(step == nx - 2, 0, nx - 1))

    lane = lax.broadcasted_iota(jnp.int32, (ny, LANES), 1)
    spans = [slice(h * LANES, (h + 1) * LANES) for h in range(halves)]

    def gathered(stage, x):
        acc = [[source[k, x, :, s] for s in spans] for k in range(nvar)]
        centres = []
        for e in range(nvar):
            centre = [fields[stage, e, x + 1, h, PAD : PAD + ny, :] for h in range(halves)]
            centres.append(centre)
            up = [pltpu.roll(c, LANES - 1, 1) for c in centre] + [jnp.zeros((ny, LANES), jnp.float32)]
            down = [jnp.zeros((ny, LANES), jnp.float32)] + [pltpu.roll(c, 1, 1) for c in centre]
            shifted = (
                [fields[stage, e, x + 2, h, PAD : PAD + ny, :] for h in range(halves)],
                [fields[stage, e, x, h, PAD : PAD + ny, :] for h in range(halves)],
                [fields[stage, e, x + 1, h, PAD + 1 : PAD + ny + 1, :] for h in range(halves)],
                [fields[stage, e, x + 1, h, PAD - 1 : PAD + ny - 1, :] for h in range(halves)],
                [jnp.where(lane == LANES - 1, up[h + 1], up[h]) for h in range(halves)],
                [jnp.where(lane == 0, down[h], down[h + 1]) for h in range(halves)],
            )
            for d in range(6):
                for k in range(nvar):
                    scale = flux[e, k, 0, d]
                    for h in range(halves):
                        acc[k][h] = acc[k][h] + scale * shifted[d][h]
        return acc, centres

    def ready(stage, step):
        x = plane_of(step)
        if stage == 0:

            @pl.when(step < nx - 2)
            def _():
                for copy in plane_loads(step + 2):
                    copy.wait()

        else:
            receive(row_copies(stage, x))

        @pl.when(step == nx - 2)
        def _():
            receive(first_x if stage == 0 else face_copies(stage))

        return x

    def relax(stage, step_index, carry):
        x = ready(stage, step_index)
        acc, centres = gathered(stage, x)
        step = [RELAX / diagonal[x, :, s] for s in spans]
        total = [None] * halves
        for k in range(nvar):
            for h in range(halves):
                value = (1.0 - RELAX) * centres[k][h] + step[h] * acc[k][h]
                fields[stage + 1, k, x + 1, h, PAD : PAD + ny, :] = value
                if stage == 1:
                    smoothed_out[0, k, x, :, spans[h]] = value
                    term = value * sensitivity[k, x, :, spans[h]].astype(jnp.float32)
                    total[h] = term if k == 0 else total[h] + term
        if stage == 1:
            for h in range(halves):
                surface[x, :, spans[h]] = total[h] * mask[x, :, spans[h]].astype(jnp.float32)
        begin(row_copies(stage + 1, x))
        up_face, down_face = face_copies(stage + 1)
        pl.when(x == nx - 1)(functools.partial(begin, [up_face]))
        pl.when(x == 0)(functools.partial(begin, [down_face]))
        return carry

    def settle(step_index, carry):
        x = ready(2, step_index)
        acc, centres = gathered(2, x)
        for k in range(nvar):
            for h in range(halves):
                value = acc[k][h] - diagonal[x, :, spans[h]] * centres[k][h]
                residual_out[0, k, x, :, spans[h]] = value
        return carry

    for x in range(2):
        for copy in plane_loads(x):
            copy.wait()
    receive(first_y)
    lax.fori_loop(0, nx, functools.partial(relax, 0), 0)
    for copy in late_loads:
        copy.wait()
    lax.fori_loop(0, nx, functools.partial(relax, 1), 0)

    def split(value):
        high = value.astype(jnp.bfloat16)
        return high, (value - high.astype(jnp.float32)).astype(jnp.bfloat16)

    dot = functools.partial(jnp.dot, preferred_element_type=jnp.float32)
    basis_high, basis_low = split(basis[...])
    surface_high, surface_low = split(surface[...].reshape(nx * ny, nz))
    projected = (
        dot(surface_high, basis_high) + dot(surface_high, basis_low) + dot(surface_low, basis_high)
    )
    lines = NDES // LANES
    line = lax.broadcasted_iota(jnp.int32, (lines, ny), 0)
    wanted = jnp.concatenate([2 * line, 2 * line + 1, 2 * line - 1], axis=0)
    looked = jnp.zeros((3 * lines, LANES), jnp.float32)
    for x in range(nx):
        onehot = (wanted == slots[x : x + 1, :]).astype(jnp.float32).astype(jnp.bfloat16)
        high, low = split(projected[x * ny : (x + 1) * ny])
        looked = looked + dot(onehot, high) + dot(onehot, low)
    turned = pltpu.roll(looked[lines:], LANES // 2, 1)
    column = lax.broadcasted_iota(jnp.int32, (lines, LANES), 1)
    gradient = looked[:lines] + jnp.where(column < LANES // 2, turned[lines:], turned[:lines])
    weight_sum = weights[0]
    for c in range(1, n_cond):
        weight_sum = weight_sum + weights[c]
    share = jnp.full((1, LANES), weights[ci], jnp.int32).astype(jnp.float32) / jnp.full(
        (1, LANES), weight_sum, jnp.int32
    ).astype(jnp.float32)
    gradient = gradient * share
    for g in range(lines // rows):
        pieces[g] = gradient[g * rows : (g + 1) * rows]

    def group(gx, yz):
        return (gx * n_yz + yz) * per_owner // (rows * LANES)

    def give(c, gx, yz):
        remote(
            pieces.at[group(gx, yz)],
            arrived.at[me],
            (piece_sems.at[0], piece_sems.at[1]),
            (c, gx, yz),
        ).start()

    arrived[me] = pieces[group(xi, yi)]
    for_others(give)
    lax.fori_loop(0, nx, settle, 0)

    others = arrived.at[pl.ds(0, devices - 1)]
    for i in range(2):
        pltpu.make_async_copy(others, others, piece_sems.at[i]).wait()
    gradient_out[...] = jnp.sum(arrived[...], axis=0)
    drain(first_y)
    drain(first_x)
    for stage in (1, 2):
        drain(face_copies(stage))

        def drain_row(x, carry, stage=stage):
            drain(row_copies(stage, x))
            return carry

        lax.fori_loop(0, nx, drain_row, 0)


def local(
    adjoint,
    objective_gradient,
    diagonal,
    flux_blocks,
    flux_sensitivity,
    surface_mask,
    patch_band_slot,
    design_basis,
    condition_weights,
):
    sizes = tuple(lax.axis_size(axis) for axis in ("cond", "gx", "yz"))
    devices = sizes[0] * sizes[1] * sizes[2]
    _, nvar, nx, ny, nz = adjoint.shape
    halves = nz // LANES
    per_owner = NDES // (sizes[1] * sizes[2])
    rows = max(1, per_owner // LANES)
    f32 = jnp.float32
    hbm = pl.BlockSpec(memory_space=pltpu.MemorySpace.HBM)
    smem = pl.BlockSpec(memory_space=pltpu.MemorySpace.SMEM)
    vmem = pl.BlockSpec(memory_space=pltpu.MemorySpace.VMEM)
    smoothed, residual, gradient = pl.pallas_call(
        functools.partial(kernel, sizes),
        out_shape=(
            pltpu.VMEM(adjoint.shape, f32),
            pltpu.VMEM(adjoint.shape, f32),
            pltpu.VMEM((rows, LANES), f32),
        ),
        in_specs=[hbm, hbm, hbm, smem, hbm, hbm, hbm, hbm, smem],
        out_specs=(vmem, vmem, vmem),
        scratch_shapes=[
            pltpu.VMEM((3, nvar, nx + 2, halves, ny + 2 * PAD, LANES), f32),
            pltpu.VMEM((nvar, nx, ny, nz), f32),
            pltpu.VMEM((nx, ny, nz), f32),
            pltpu.VMEM((nvar, nx, ny, nz), jnp.bfloat16),
            pltpu.VMEM((nx, ny, nz), jnp.int32),
            pltpu.VMEM((nx, ny), jnp.int32),
            pltpu.VMEM(design_basis.shape, f32),
            pltpu.VMEM((nx, ny, nz), f32),
            pltpu.VMEM((NDES // (rows * LANES), rows, LANES), f32),
            pltpu.VMEM((devices, rows, LANES), f32),
            pltpu.SemaphoreType.DMA((4,)),
            pltpu.SemaphoreType.DMA((2 + halves, nx)),
            pltpu.SemaphoreType.DMA((2, 4, halves)),
            pltpu.SemaphoreType.DMA((2, 2, 2, nx)),
            pltpu.SemaphoreType.DMA((2, 2, 2)),
            pltpu.SemaphoreType.DMA((2,)),
        ],
        compiler_params=pltpu.CompilerParams(
            collective_id=0, has_side_effects=True, vmem_limit_bytes=67043328 - 2 * adjoint.size * 4 - 2**16
        ),
    )(
        adjoint,
        objective_gradient,
        diagonal,
        jnp.transpose(flux_blocks, (2, 3, 0, 1)),
        flux_sensitivity,
        surface_mask,
        patch_band_slot,
        design_basis,
        condition_weights,
    )
    flat = gradient.reshape(-1)
    if per_owner < flat.shape[0]:
        owner = lax.axis_index(("gx", "yz"))
        flat = lax.dynamic_slice_in_dim(flat, (owner * per_owner) % flat.shape[0], per_owner, 0)
    return smoothed, residual, flat


def solution(mesh):
    placed = (
        P("cond", None, "gx", "yz", None),
        P("cond", None, "gx", "yz", None),
        P("gx", "yz", None),
        P("cond", None, None, None),
        P("cond", None, "gx", "yz", None),
        P("gx", "yz", None),
        P("gx", "yz"),
        P(),
        P(),
    )
    return jax.shard_map(
        local,
        mesh=mesh,
        in_specs=placed,
        out_specs=(
            P("cond", None, "gx", "yz", None),
            P("cond", None, "gx", "yz", None),
            P(("gx", "yz")),
        ),
        check_vma=False,
    )
```

profile of v0, /device:TPU:0, one launch (start us, length us, event | category | flops | bytes accessed | tf_op | source)
XLA Modules:
  0.0 24.3 jit_solution(15123942980295389175)
XLA Ops:
  0.6 21.4 %shard_map.112 = (f32[1,5,8,16,256]{4,3,2,1,0:T(8,128)S(1)}, f32[1,5,8,16,256]{4,3,2,1,0:T(8,128)S(1)}, f32[2,128]{1,0:T(2,128)S(1)}) custom-call(f32[1,5,8,16,256]{4,3,2,1,0:T(8,128)} %adjoint.1, f32[1,5,8,16,256]{4,3,2,1,0:T(8,128)} %source_hbm.1, f32[8,16,256]{2,1,0:T(8,128)} %diagonal_hbm.1, f32[5,5,1,6]{3,2,1,0:T(1,128)} %bitcast.3, ...), custom_call_target="tpu_custom_call" | custom-call | tf_op jit(solution)/shard_map/pallas_call | solution.py:379
  22.0 0.8 %copy.15 = f32[1,5,8,16,256]{4,3,2,1,0:T(8,128)} copy(f32[1,5,8,16,256]{4,3,2,1,0:T(8,128)S(1)} %get-tuple-element.9) | data formatting | bytes 1310720
  22.9 0.6 %copy.17 = f32[256]{0:T(256)} copy(f32[256]{0:T(256)S(1)} %bitcast.2) | data formatting | bytes 2048
  23.4 0.8 %copy.16 = f32[1,5,8,16,256]{4,3,2,1,0:T(8,128)} copy(f32[1,5,8,16,256]{4,3,2,1,0:T(8,128)S(1)} %get-tuple-element.10) | data formatting | bytes 1310720
where the time goes:
time: 24.5 us; the launch traced here: 24.3 us
  Pallas kernels  21.4 us (87%)
  local copies, waits for them, and re-layouts  2.24 us (9%)
  between operations  0.64 us (3%)
    pallas_call x1, Pallas kernels, local(): pl.pallas_call(functools.partial(kernel, sizes), out_shape=(pltpu.VMEM(ad...  21.4 us
    unnamed x3, local copies, waits for them, and re-layouts  2.24 us

commit v1 on v0

v1 whole, which is shorter than its diff:
```python
import functools

import jax
import jax.numpy as jnp
from jax import lax
from jax.experimental import pallas as pl
from jax.experimental.pallas import tpu as pltpu
from jax.sharding import PartitionSpec as P

NDES = 4096
RELAX = 0.8
LANES = 128
PAD = 8
MESH = pl.DeviceIdType.MESH


def spans_of(count):
    reach, out = 1, []
    while reach < count - 1:
        out.append(reach)
        reach *= 2
    return out


def kernel(
    sizes,
    adjoint,
    source_hbm,
    diagonal_hbm,
    flux_hbm,
    sensitivity_hbm,
    mask_hbm,
    slots_hbm,
    basis_hbm,
    weights_hbm,
    smoothed_out,
    residual_out,
    gradient_out,
    fields,
    source,
    diagonal,
    flux,
    sensitivity,
    mask,
    slots,
    basis,
    weights,
    surface,
    edges,
    row_halo,
    face_halo,
    step_edge,
    weight_edge,
    onehot,
    pieces,
    arrived,
    scalar_sems,
    local_sems,
    adjoint_sems,
    plane_sems,
    row_sems,
    face_sems,
    piece_sems,
    round_sems,
):
    n_cond, n_gx, n_yz = sizes
    devices = n_cond * n_gx * n_yz
    nvar, nx, ny, nz = source.shape
    halves = nz // LANES
    rows = pieces.shape[1]
    per_owner = NDES // (n_gx * n_yz)
    lines = NDES // LANES
    ci, xi, yi = lax.axis_index("cond"), lax.axis_index("gx"), lax.axis_index("yz")
    me = (ci * n_gx + xi) * n_yz + yi
    has_before_x, has_after_x = xi > 0, xi < n_gx - 1
    has_before_y, has_after_y = yi > 0, yi < n_yz - 1
    after_x, before_x = (ci, xi + 1, yi), (ci, xi - 1, yi)
    after_y, before_y = (ci, xi, yi + 1), (ci, xi, yi - 1)

    def signal(sem, target):
        pl.semaphore_signal(sem, inc=1, device_id=target, device_id_type=MESH)

    barrier = pltpu.get_barrier_semaphore()
    beside = n_cond - 1
    for there, target in (
        (has_before_x, before_x),
        (has_after_x, after_x),
        (has_before_y, before_y),
        (has_after_y, after_y),
    ):
        pl.when(there)(functools.partial(signal, barrier, target))
        beside = beside + there.astype(jnp.int32)
    for t in range(1, n_cond):
        signal(barrier, ((ci + t) % n_cond, xi, yi))

    spans = [slice(h * LANES, (h + 1) * LANES) for h in range(halves)]
    inner_y = pl.ds(PAD, ny)

    scalar_loads = [
        pltpu.make_async_copy(flux_hbm, flux, scalar_sems.at[0]),
        pltpu.make_async_copy(weights_hbm, weights, scalar_sems.at[1]),
    ]
    adjoint_loads = [
        pltpu.make_async_copy(
            adjoint.at[0, k, :, :, pl.ds(h * LANES, LANES)],
            fields.at[0, k, pl.ds(1, nx), h, inner_y, :],
            adjoint_sems.at[k, h],
        )
        for k in range(nvar)
        for h in range(halves)
    ]

    def plane_loads(x):
        return [
            pltpu.make_async_copy(source_hbm.at[0, :, x], source.at[:, x], plane_sems.at[0, x]),
            pltpu.make_async_copy(diagonal_hbm.at[x], diagonal.at[x], plane_sems.at[1, x]),
        ]

    late_loads = [
        pltpu.make_async_copy(src, dst, local_sems.at[i])
        for i, (src, dst) in enumerate(
            (
                (sensitivity_hbm.at[0], sensitivity),
                (mask_hbm, mask),
                (slots_hbm, slots),
                (basis_hbm, basis),
            )
        )
    ]
    for copy in adjoint_loads:
        copy.start()
    for copy in scalar_loads:
        copy.start()
    for x in range(nx):
        for copy in plane_loads(x):
            copy.start()
    for copy in late_loads:
        copy.start()

    blank = jnp.zeros((nvar, halves, ny, LANES), jnp.float32)
    blank_row = jnp.zeros((nvar, nx, halves, 1, LANES), jnp.float32)

    def outer(stage):
        return smoothed_out if stage == 2 else fields.at[stage]

    for stage in range(3):
        field = outer(stage)
        for x in (0, nx + 1):
            field[:, x, :, PAD : PAD + ny, :] = blank
        for y in (PAD - 1, PAD + ny):
            field[:, 1 : nx + 1, :, y : y + 1, :] = blank_row

    def clear_face(side):
        for stage in range(3):
            face_halo[stage, side] = blank

    def clear_row(side):
        for stage in range(3):
            row_halo[stage, side] = jnp.zeros((nvar, halves, nx, LANES), jnp.float32)

    pl.when(xi == 0)(functools.partial(clear_face, 0))
    pl.when(xi == n_gx - 1)(functools.partial(clear_face, 1))
    pl.when(yi == 0)(functools.partial(clear_row, 0))
    pl.when(yi == n_yz - 1)(functools.partial(clear_row, 1))

    def remote(src, dst, sems, target):
        return pltpu.make_async_remote_copy(
            src_ref=src,
            dst_ref=dst,
            send_sem=sems[0],
            recv_sem=sems[1],
            device_id=target,
            device_id_type=MESH,
        )

    def copies(stage):
        def face(x):
            return outer(stage).at[:, x, :, inner_y, :]

        def sems(ref, way):
            return ref.at[stage, 0, way], ref.at[stage, 1, way]

        up_x = remote(face(nx), face_halo.at[stage, 0], sems(face_sems, 0), after_x)
        down_x = remote(face(1), face_halo.at[stage, 1], sems(face_sems, 1), before_x)
        up_y = remote(edges.at[stage, 1], row_halo.at[stage, 0], sems(row_sems, 0), after_y)
        down_y = remote(edges.at[stage, 0], row_halo.at[stage, 1], sems(row_sems, 1), before_y)
        return (
            [(has_after_x, has_before_x, up_x), (has_before_x, has_after_x, down_x)],
            [(has_after_y, has_before_y, up_y), (has_before_y, has_after_y, down_y)],
        )

    def begin(plans):
        for go, _, copy in plans:
            pl.when(go)(copy.start)

    def receive(plans):
        for _, come, copy in plans:
            pl.when(come)(copy.wait_recv)

    def drain(plans):
        for go, _, copy in plans:
            pl.when(go)(copy.wait_send)

    def line_round(distances):
        targets = []
        for axis, distance in distances:
            here, count = (xi, n_gx) if axis == "gx" else (yi, n_yz)
            for sign in (1, -1):
                there = here + sign * distance
                target = (ci, there, yi) if axis == "gx" else (ci, xi, there)
                targets.append((jnp.logical_and(there >= 0, there < count), target))
        return targets

    gx_spans, yz_spans = spans_of(n_gx), spans_of(n_yz)
    rounds = []
    for i in range(max(len(gx_spans), len(yz_spans))):
        distances = [("gx", d) for d in gx_spans[i : i + 1]] + [("yz", d) for d in yz_spans[i : i + 1]]
        rounds.append(line_round(distances))
    always = ci >= 0
    rounds.append([(always, (ci, (xi + t) % n_gx, yi)) for t in range(1, n_gx)])
    rounds.append([(always, ((ci + t) % n_cond, xi, yi)) for t in range(1, n_cond)])

    def tell(i):
        for there, target in rounds[i]:
            pl.when(there)(functools.partial(signal, round_sems.at[i], target))

    def hear(i):
        count = 0
        for there, _ in rounds[i]:
            count = count + there.astype(jnp.int32)
        pl.semaphore_wait(round_sems.at[i], count)

    def advance(i):
        hear(i)
        if i + 1 < len(rounds):
            tell(i + 1)

    for copy in adjoint_loads:
        copy.wait()
    for x in range(nx):
        for k in range(nvar):
            for h in range(halves):
                edges[0, 0, k, h, x : x + 1, :] = fields[0, k, x + 1, h, PAD : PAD + 1, :]
                last = PAD + ny - 1
                edges[0, 1, k, h, x : x + 1, :] = fields[0, k, x + 1, h, last : last + 1, :]
    pl.semaphore_wait(barrier, beside)
    for plans in copies(0):
        begin(plans)
    tell(0)
    for copy in scalar_loads:
        copy.wait()

    lane = lax.broadcasted_iota(jnp.int32, (ny, LANES), 1)

    def gathered(stage, x):
        field = outer(stage)
        acc = [[source[k, x, :, s] for s in spans] for k in range(nvar)]
        centres = []
        for e in range(nvar):
            centre = [field[e, x + 1, h, PAD : PAD + ny, :] for h in range(halves)]
            centres.append(centre)
            up = [pltpu.roll(c, LANES - 1, 1) for c in centre] + [jnp.zeros((ny, LANES), jnp.float32)]
            down = [jnp.zeros((ny, LANES), jnp.float32)] + [pltpu.roll(c, 1, 1) for c in centre]
            shifted = (
                [field[e, x + 2, h, PAD : PAD + ny, :] for h in range(halves)],
                [field[e, x, h, PAD : PAD + ny, :] for h in range(halves)],
                [field[e, x + 1, h, PAD + 1 : PAD + ny + 1, :] for h in range(halves)],
                [field[e, x + 1, h, PAD - 1 : PAD + ny - 1, :] for h in range(halves)],
                [jnp.where(lane == LANES - 1, up[h + 1], up[h]) for h in range(halves)],
                [jnp.where(lane == 0, down[h], down[h + 1]) for h in range(halves)],
            )
            for d in range(6):
                for k in range(nvar):
                    scale = flux[e, k, 0, d]
                    for h in range(halves):
                        acc[k][h] = acc[k][h] + scale * shifted[d][h]
        return acc, centres

    def keep_edges(stage, k, h, x, value):
        edges[stage, 0, k, h, pl.ds(x, 1), :] = value[0:1]
        edges[stage, 1, k, h, pl.ds(x, 1), :] = value[ny - 1 : ny]

    def relax(stage, x, carry):
        if stage == 0:
            for copy in plane_loads(x):
                copy.wait()
        acc, centres = gathered(stage, x)
        step = [RELAX / diagonal[x, :, s] for s in spans]
        total = [None] * halves
        for h in range(halves):
            if stage == 0:
                step_edge[0, h, pl.ds(x, 1), :] = step[h][0:1]
                step_edge[1, h, pl.ds(x, 1), :] = step[h][ny - 1 : ny]
            else:
                cover = mask[x, :, spans[h]].astype(jnp.float32)
            for k in range(nvar):
                value = (1.0 - RELAX) * centres[k][h] + step[h] * acc[k][h]
                outer(stage + 1)[k, x + 1, h, PAD : PAD + ny, :] = value
                keep_edges(stage + 1, k, h, x, value)
                if stage == 1:
                    weight = sensitivity[k, x, :, spans[h]].astype(jnp.float32) * cover
                    weight_edge[0, k, h, pl.ds(x, 1), :] = weight[0:1]
                    weight_edge[1, k, h, pl.ds(x, 1), :] = weight[ny - 1 : ny]
                    term = value * weight
                    total[h] = term if k == 0 else total[h] + term
            if stage == 1:
                surface[x, :, spans[h]] = total[h]
        return carry

    def settle(x, carry):
        acc, centres = gathered(2, x)
        for k in range(nvar):
            for h in range(halves):
                value = acc[k][h] - diagonal[x, :, spans[h]] * centres[k][h]
                residual_out[0, k, x, :, spans[h]] = value
                keep_edges(3, k, h, x, value)
        return carry

    def brought(halo, h, d):
        cells = [halo[e, h] for e in range(nvar)]
        out = []
        for k in range(nvar):
            total = flux[0, k, 0, d] * cells[0]
            for e in range(1, nvar):
                total = total + flux[e, k, 0, d] * cells[e]
            out.append(total)
        return out

    def add_faces(stage):
        for side, x, d in ((0, 0, 1), (1, nx - 1, 0)):
            for h in range(halves):
                more = brought(face_halo.at[stage, side], h, d)
                if stage < 2:
                    step = RELAX / diagonal[x, :, spans[h]]
                total = None
                for k in range(nvar):
                    if stage == 2:
                        value = residual_out[0, k, x, :, spans[h]] + more[k]
                        residual_out[0, k, x, :, spans[h]] = value
                    else:
                        part = step * more[k]
                        value = outer(stage + 1)[k, x + 1, h, PAD : PAD + ny, :] + part
                        outer(stage + 1)[k, x + 1, h, PAD : PAD + ny, :] = value
                        if stage == 1:
                            term = part * sensitivity[k, x, :, spans[h]].astype(jnp.float32)
                            total = term if k == 0 else total + term
                    keep_edges(stage + 1, k, h, x, value)
                if stage == 1:
                    cover = mask[x, :, spans[h]].astype(jnp.float32)
                    surface[x, :, spans[h]] = surface[x, :, spans[h]] + total * cover

    def add_rows(stage):
        for side, y, d in ((0, 0, 3), (1, ny - 1, 2)):
            for h in range(halves):
                more = brought(row_halo.at[stage, side], h, d)
                total = None
                for k in range(nvar):
                    part = more[k] if stage == 2 else step_edge[side, h] * more[k]
                    value = edges[stage + 1, side, k, h] + part
                    if stage < 2:
                        edges[stage + 1, side, k, h] = value
                    if stage == 1:
                        term = part * weight_edge[side, k, h]
                        total = term if k == 0 else total + term
                    for x in range(nx):
                        if stage == 2:
                            residual_out[0, k, x, y : y + 1, spans[h]] = value[x : x + 1]
                        else:
                            outer(stage + 1)[k, x + 1, h, PAD + y : PAD + y + 1, :] = value[x : x + 1]
                if stage == 1:
                    for x in range(nx):
                        line = surface[x, y : y + 1, spans[h]]
                        surface[x, y : y + 1, spans[h]] = line + total[x : x + 1]

    def complete(stage):
        faces, ranks = copies(stage)
        receive(faces)
        add_faces(stage)
        receive(ranks)
        add_rows(stage)

    lax.fori_loop(0, nx, functools.partial(relax, 0), 0)
    advance(0)
    complete(0)
    for plans in copies(1):
        begin(plans)
    for i in range(1, len(rounds) - 2):
        advance(i)

    for copy in late_loads:
        copy.wait()

    def relax_and_advance(x, carry):
        relax(1, x, carry)

        @pl.when(x == nx // 2)
        def _():
            advance(len(rounds) - 2)

        return carry

    lax.fori_loop(0, nx, relax_and_advance, 0)

    def split(value):
        high = value.astype(jnp.bfloat16)
        return high, (value - high.astype(jnp.float32)).astype(jnp.bfloat16)

    line = lax.broadcasted_iota(jnp.int32, (lines, nx * ny), 0)
    spots = jnp.concatenate([slots[x : x + 1, :] for x in range(nx)], axis=1)
    wanted = jnp.concatenate([2 * line, 2 * line + 1, 2 * line - 1], axis=0)
    onehot[...] = (wanted == spots).astype(jnp.float32).astype(jnp.bfloat16)
    weight_sum = weights[0]
    for c in range(1, n_cond):
        weight_sum = weight_sum + weights[c]
    share = jnp.full((1, LANES), weights[ci], jnp.int32).astype(jnp.float32) / jnp.full(
        (1, LANES), weight_sum, jnp.int32
    ).astype(jnp.float32)

    complete(1)
    for plans in copies(2):
        begin(plans)

    dot = functools.partial(jnp.dot, preferred_element_type=jnp.float32)
    basis_high, basis_low = split(basis[...])
    surface_high, surface_low = split(surface[...].reshape(nx * ny, nz))
    projected = (
        dot(surface_high, basis_high) + dot(surface_high, basis_low) + dot(surface_low, basis_high)
    )
    high, low = split(projected)
    looked = dot(onehot[...], high) + dot(onehot[...], low)
    turned = pltpu.roll(looked[lines:], LANES // 2, 1)
    column = lax.broadcasted_iota(jnp.int32, (lines, LANES), 1)
    gradient = looked[:lines] + jnp.where(column < LANES // 2, turned[lines:], turned[:lines])
    gradient = gradient * share
    for g in range(lines // rows):
        pieces[g] = gradient[g * rows : (g + 1) * rows]

    def group(gx, yz):
        return (gx * n_yz + yz) * per_owner // (rows * LANES)

    def give(c, gx, yz):
        remote(
            pieces.at[group(gx, yz)],
            arrived.at[me],
            (piece_sems.at[0], piece_sems.at[1]),
            (c, gx, yz),
        ).start()

    arrived[me] = pieces[group(xi, yi)]
    advance(len(rounds) - 1)
    if devices <= 64:
        for dy in range(n_yz):
            for dx in range(n_gx):
                for dc in range(n_cond):
                    if dc or dx or dy:
                        give((ci + dc) % n_cond, (xi + dx) % n_gx, (yi + dy) % n_yz)
    else:

        def give_next(t, carry):
            flat = (me + t) % devices
            give(flat // (n_gx * n_yz), (flat // n_yz) % n_gx, flat % n_yz)
            return carry

        lax.fori_loop(1, devices, give_next, 0)

    lax.fori_loop(0, nx, settle, 0)
    others = arrived.at[pl.ds(0, devices - 1)]
    for i in range(2):
        pltpu.make_async_copy(others, others, piece_sems.at[i]).wait()
    gradient_out[...] = jnp.sum(arrived[...], axis=0)
    complete(2)
    for stage in range(3):
        for plans in copies(stage):
            drain(plans)


def write(padded, residual, gradient, smoothed_hbm, residual_hbm, gradient_hbm, sems):
    nvar, planes, halves = padded.shape[:3]
    nx, ny = planes - 2, smoothed_hbm.shape[3]
    stores = [
        pltpu.make_async_copy(
            padded.at[:, pl.ds(1, nx), h, pl.ds(PAD, ny), :],
            smoothed_hbm.at[0, :, :, :, pl.ds(h * LANES, LANES)],
            sems.at[2 + h],
        )
        for h in range(halves)
    ]
    stores.append(pltpu.make_async_copy(residual, residual_hbm, sems.at[0]))
    stores.append(pltpu.make_async_copy(gradient, gradient_hbm, sems.at[1]))
    for copy in stores:
        copy.start()
    for copy in stores:
        copy.wait()


def local(
    adjoint,
    objective_gradient,
    diagonal,
    flux_blocks,
    flux_sensitivity,
    surface_mask,
    patch_band_slot,
    design_basis,
    condition_weights,
):
    sizes = tuple(lax.axis_size(axis) for axis in ("cond", "gx", "yz"))
    devices = sizes[0] * sizes[1] * sizes[2]
    _, nvar, nx, ny, nz = adjoint.shape
    halves = nz // LANES
    per_owner = NDES // (sizes[1] * sizes[2])
    rows = max(1, per_owner // LANES)
    lines = NDES // LANES
    rounds = max(len(spans_of(sizes[1])), len(spans_of(sizes[2]))) + 2
    f32 = jnp.float32
    hbm = pl.BlockSpec(memory_space=pltpu.MemorySpace.HBM)
    vmem = pl.BlockSpec(memory_space=pltpu.MemorySpace.VMEM)
    padded = (nvar, nx + 2, halves, ny + 2 * PAD, LANES)
    grant = 67043328 - 2**16 - 4 * (adjoint.size + 2 * adjoint.size * (nx + 2) * (ny + 2 * PAD) // (nx * ny))
    smoothed, residual, gradient = pl.pallas_call(
        functools.partial(kernel, sizes),
        out_shape=(
            pltpu.VMEM(padded, f32),
            pltpu.VMEM(adjoint.shape, f32),
            pltpu.VMEM((rows, LANES), f32),
        ),
        in_specs=[hbm] * 9,
        out_specs=(vmem, vmem, vmem),
        scratch_shapes=[
            pltpu.VMEM((2,) + padded, f32),
            pltpu.VMEM((nvar, nx, ny, nz), f32),
            pltpu.VMEM((nx, ny, nz), f32),
            pltpu.SMEM((nvar, nvar, 1, 6), f32),
            pltpu.VMEM((nvar, nx, ny, nz), jnp.bfloat16),
            pltpu.VMEM((nx, ny, nz), jnp.int32),
            pltpu.VMEM((nx, ny), jnp.int32),
            pltpu.VMEM(design_basis.shape, f32),
            pltpu.SMEM(condition_weights.shape, jnp.int32),
            pltpu.VMEM((nx, ny, nz), f32),
            pltpu.VMEM((4, 2, nvar, halves, nx, LANES), f32),
            pltpu.VMEM((3, 2, nvar, halves, nx, LANES), f32),
            pltpu.VMEM((3, 2, nvar, halves, ny, LANES), f32),
            pltpu.VMEM((2, halves, nx, LANES), f32),
            pltpu.VMEM((2, nvar, halves, nx, LANES), f32),
            pltpu.VMEM((3 * lines, nx * ny), jnp.bfloat16),
            pltpu.VMEM((NDES // (rows * LANES), rows, LANES), f32),
            pltpu.VMEM((devices, rows, LANES), f32),
            pltpu.SemaphoreType.DMA((2,)),
            pltpu.SemaphoreType.DMA((4,)),
            pltpu.SemaphoreType.DMA((nvar, halves)),
            pltpu.SemaphoreType.DMA((2, nx)),
            pltpu.SemaphoreType.DMA((3, 2, 2)),
            pltpu.SemaphoreType.DMA((3, 2, 2)),
            pltpu.SemaphoreType.DMA((2,)),
            pltpu.SemaphoreType.REGULAR((rounds,)),
        ],
        compiler_params=pltpu.CompilerParams(
            collective_id=0, has_side_effects=True, vmem_limit_bytes=grant
        ),
    )(
        adjoint,
        objective_gradient,
        diagonal,
        jnp.transpose(flux_blocks, (2, 3, 0, 1)),
        flux_sensitivity,
        surface_mask,
        patch_band_slot,
        design_basis,
        condition_weights,
    )
    smoothed, residual, gradient = pl.pallas_call(
        write,
        out_shape=(
            jax.ShapeDtypeStruct(adjoint.shape, f32),
            jax.ShapeDtypeStruct(adjoint.shape, f32),
            jax.ShapeDtypeStruct((rows, LANES), f32),
        ),
        in_specs=[vmem] * 3,
        out_specs=(hbm, hbm, hbm),
        scratch_shapes=[pltpu.SemaphoreType.DMA((2 + halves,))],
    )(smoothed, residual, gradient)
    flat = gradient.reshape(-1)
    if per_owner < flat.shape[0]:
        owner = lax.axis_index(("gx", "yz"))
        flat = lax.dynamic_slice_in_dim(flat, (owner * per_owner) % flat.shape[0], per_owner, 0)
    return smoothed, residual, flat


def solution(mesh):
    placed = (
        P("cond", None, "gx", "yz", None),
        P("cond", None, "gx", "yz", None),
        P("gx", "yz", None),
        P("cond", None, None, None),
        P("cond", None, "gx", "yz", None),
        P("gx", "yz", None),
        P("gx", "yz"),
        P(),
        P(),
    )
    return jax.shard_map(
        local,
        mesh=mesh,
        in_specs=placed,
        out_specs=(
            P("cond", None, "gx", "yz", None),
            P("cond", None, "gx", "yz", None),
            P(("gx", "yz")),
        ),
        check_vma=False,
    )
```

time: 24.5 us -> 23.7 us (0.967)
  Pallas kernels: 21.4 us -> 20.3 us
  local copies, waits for them, and re-layouts: 2.24 us -> 2.62 us
    pallas_call x1 -> x2, Pallas kernels: 21.4 us -> 20.3 us  [the longest x1 17.5 us: local(): pl.pallas_call(functools.partial(kernel, sizes), out_shape=(pltpu.VMEM(pa...]
    unnamed x3 -> x6, local copies, waits for them, and re-layouts: 2.24 us -> 2.62 us
where the time goes in v1:
time: 23.7 us; the launch traced here: 23.5 us
  Pallas kernels  20.3 us (86%)
  local copies, waits for them, and re-layouts  2.62 us (11%)
  between operations  0.65 us (3%)
    pallas_call x1, Pallas kernels, local(): pl.pallas_call(functools.partial(kernel, sizes), out_shape=(pltpu.VMEM(pa...  17.5 us
    pallas_call x1, Pallas kernels, local(): pl.pallas_call(write, out_shape=(jax.ShapeDtypeStruct(adjoint.shape, f32)...  2.73 us
    unnamed x6, local copies, waits for them, and re-layouts  2.62 us

profile of v1, /device:TPU:0, one launch (start us, length us, event | category | flops | bytes accessed | tf_op | source)
XLA Modules:
  0.0 23.5 jit_solution(17633350914692999459)
XLA Ops:
  0.6 17.5 %shard_map.112 = (f32[5,10,2,32,128]{4,3,2,1,0:T(8,128)S(1)}, f32[1,5,8,16,256]{4,3,2,1,0:T(8,128)S(1)}, f32[2,128]{1,0:T(2,128)S(1)}) custom-call(f32[1,5,8,16,256]{4,3,2,1,0:T(8,128)} %adjoint.1, f32[1,5,8,16,256]{4,3,2,1,0:T(8,128)} %source_hbm.1, f32[8,16,256]{2,1,0:T(8,128)} %diagonal_hbm.1, f32[5,5,1,6]{3,2,1,0:T(1,128)} %bitcast.2, ...), custom_call_target="tpu_custom_call" | custom-call | tf_op jit(solution)/shard_map/pallas_call | solution.py:520
  18.2 0.0 copy-start
  18.2 1.2 %copy-done = f32[5,10,2,32,128]{4,3,2,1,0:T(8,128)} copy-done((f32[5,10,2,32,128]{4,3,2,1,0:T(8,128)}, f32[5,10,2,32,128]{4,3,2,1,0:T(8,128)S(1)}, u32[]{:S(2)}) %copy-start) | copy-done | bytes 1638424
  19.3 0.0 copy-start.1
  19.3 0.9 %copy-done.1 = f32[1,5,8,16,256]{4,3,2,1,0:T(8,128)} copy-done((f32[1,5,8,16,256]{4,3,2,1,0:T(8,128)}, f32[1,5,8,16,256]{4,3,2,1,0:T(8,128)S(1)}, u32[]{:S(2)}) %copy-start.1) | copy-done | bytes 655384
  20.2 0.0 copy-start.2
  20.2 0.6 %copy-done.2 = f32[2,128]{1,0:T(2,128)} copy-done((f32[2,128]{1,0:T(2,128)}, f32[2,128]{1,0:T(2,128)S(1)}, u32[]{:S(2)}) %copy-start.2) | copy-done | bytes 1048
  20.8 2.7 %shard_map.113 = (f32[1,5,8,16,256]{4,3,2,1,0:T(8,128)}, f32[1,5,8,16,256]{4,3,2,1,0:T(8,128)}, f32[2,128]{1,0:T(2,128)}) custom-call(f32[5,10,2,32,128]{4,3,2,1,0:T(8,128)} %copy-done, f32[1,5,8,16,256]{4,3,2,1,0:T(8,128)} %copy-done.1, f32[2,128]{1,0:T(2,128)} %copy-done.2), custom_call_target="tpu_custom_call" | custom-call | tf_op jit(solution)/shard_map/pallas_call | solution.py:571
Async XLA Ops:
  18.2 1.2 %copy-start = (f32[5,10,2,32,128]{4,3,2,1,0:T(8,128)}, f32[5,10,2,32,128]{4,3,2,1,0:T(8,128)S(1)}, u32[]{:S(2)}) copy-start(f32[5,10,2,32,128]{4,3,2,1,0:T(8,128)S(1)} %get-tuple-element.9.padded) | copy-start | bytes 4915204
  19.3 0.9 %copy-start.1 = (f32[1,5,8,16,256]{4,3,2,1,0:T(8,128)}, f32[1,5,8,16,256]{4,3,2,1,0:T(8,128)S(1)}, u32[]{:S(2)}) copy-start(f32[1,5,8,16,256]{4,3,2,1,0:T(8,128)S(1)} %get-tuple-element.10.residual) | copy-start | bytes 1966084
  20.2 0.6 %copy-start.2 = (f32[2,128]{1,0:T(2,128)}, f32[2,128]{1,0:T(2,128)S(1)}, u32[]{:S(2)}) copy-start(f32[2,128]{1,0:T(2,128)S(1)} %get-tuple-element.11.gradient) | copy-start | bytes 3076

commit v2 on v1

--- a/solution.py
+++ b/solution.py
@@ -578,6 +578,7 @@
         in_specs=[vmem] * 3,
         out_specs=(hbm, hbm, hbm),
         scratch_shapes=[pltpu.SemaphoreType.DMA((2 + halves,))],
+        compiler_params=pltpu.CompilerParams(vmem_limit_bytes=2**20),
     )(smoothed, residual, gradient)
     flat = gradient.reshape(-1)
     if per_owner < flat.shape[0]:

time: 23.7 us -> 19.4 us (0.82)
  local copies, waits for them, and re-layouts: 2.62 us -> 0 us
  Pallas kernels: 20.3 us -> 18.6 us
    unnamed x6 -> x0, local copies, waits for them, and re-layouts: 2.62 us -> none
    pallas_call x1, Pallas kernels: 2.73 us -> 1.09 us  [local(): pl.pallas_call(write, out_shape=(jax.ShapeDtypeStruct(adjoint.shape, f32)...]
where the time goes in v2:
time: 19.4 us; the launch traced here: 19.3 us
  Pallas kernels  18.6 us (96%)
  between operations  0.64 us (3%)
    pallas_call x1, Pallas kernels, local(): pl.pallas_call(functools.partial(kernel, sizes), out_shape=(pltpu.VMEM(pa...  17.5 us
    pallas_call x1, Pallas kernels, local(): pl.pallas_call(write, out_shape=(jax.ShapeDtypeStruct(adjoint.shape, f32)...  1.09 us

profile of v2, /device:TPU:0, one launch (start us, length us, event | category | flops | bytes accessed | tf_op | source)
XLA Modules:
  0.0 19.3 jit_solution(11011884175310056010)
XLA Ops:
  0.6 17.5 %shard_map.112 = (f32[5,10,2,32,128]{4,3,2,1,0:T(8,128)S(1)}, f32[1,5,8,16,256]{4,3,2,1,0:T(8,128)S(1)}, f32[2,128]{1,0:T(2,128)S(1)}) custom-call(f32[1,5,8,16,256]{4,3,2,1,0:T(8,128)} %adjoint.1, f32[1,5,8,16,256]{4,3,2,1,0:T(8,128)} %source_hbm.1, f32[8,16,256]{2,1,0:T(8,128)} %diagonal_hbm.1, f32[5,5,1,6]{3,2,1,0:T(1,128)} %bitcast.2, ...), custom_call_target="tpu_custom_call" | custom-call | tf_op jit(solution)/shard_map/pallas_call | solution.py:520
  18.2 1.1 %shard_map.113 = (f32[1,5,8,16,256]{4,3,2,1,0:T(8,128)}, f32[1,5,8,16,256]{4,3,2,1,0:T(8,128)}, f32[2,128]{1,0:T(2,128)}) custom-call(f32[5,10,2,32,128]{4,3,2,1,0:T(8,128)S(1)} %get-tuple-element.9.padded, f32[1,5,8,16,256]{4,3,2,1,0:T(8,128)S(1)} %get-tuple-element.10.residual, f32[2,128]{1,0:T(2,128)S(1)} %get-tuple-element.11.gradient), custom_call_target="tpu_custom_call" | custom-call | tf_op jit(solution)/shard_map/pallas_call | solution.py:571

commit v3 on v2

v3 whole, which is shorter than its diff:
```python
import functools

import jax
import jax.numpy as jnp
from jax import lax
from jax.experimental import pallas as pl
from jax.experimental.pallas import tpu as pltpu
from jax.sharding import PartitionSpec as P

NDES = 4096
RELAX = 0.8
LANES = 128
PAD = 8
MESH = pl.DeviceIdType.MESH


def spans_of(count):
    reach, out = 1, []
    while reach < count - 1:
        out.append(reach)
        reach *= 2
    return out


def kernel(
    sizes,
    adjoint,
    source_hbm,
    diagonal_hbm,
    flux_hbm,
    sensitivity_hbm,
    mask_hbm,
    slots_hbm,
    basis_hbm,
    weights_hbm,
    smoothed_out,
    residual_out,
    gradient_out,
    first,
    second,
    source,
    step_of,
    bands,
    parts,
    products,
    flux,
    sensitivity,
    mask,
    slots,
    basis,
    weights,
    surface,
    edges,
    row_true,
    face_sent,
    row_halo,
    face_halo,
    corner,
    row_more,
    face_more,
    step_edge,
    weight_edge,
    onehot,
    pieces,
    arrived,
    scalar_sems,
    local_sems,
    adjoint_sems,
    plane_sems,
    row_sems,
    face_sems,
    corner_sems,
    piece_sems,
    round_sems,
):
    n_cond, n_gx, n_yz = sizes
    devices = n_cond * n_gx * n_yz
    nvar, nx, ny, nz = source.shape
    block = nvar * ny
    rows = pieces.shape[1]
    per_owner = NDES // (n_gx * n_yz)
    lines = NDES // LANES
    ci, xi, yi = lax.axis_index("cond"), lax.axis_index("gx"), lax.axis_index("yz")
    me = (ci * n_gx + xi) * n_yz + yi
    has_before_x, has_after_x = xi > 0, xi < n_gx - 1
    has_before_y, has_after_y = yi > 0, yi < n_yz - 1
    after_x, before_x = (ci, xi + 1, yi), (ci, xi - 1, yi)
    after_y, before_y = (ci, xi, yi + 1), (ci, xi, yi - 1)

    def signal(sem, target):
        pl.semaphore_signal(sem, inc=1, device_id=target, device_id_type=MESH)

    barrier = pltpu.get_barrier_semaphore()
    around = [
        (has_before_x, before_x),
        (has_after_x, after_x),
        (has_before_y, before_y),
        (has_after_y, after_y),
    ]
    diagonals = []
    for xs, there_x in ((-1, has_before_x), (1, has_after_x)):
        for ys, there_y in ((-1, has_before_y), (1, has_after_y)):
            diagonals.append((jnp.logical_and(there_x, there_y), (ci, xi + xs, yi + ys)))
    beside = n_cond - 1
    for there, target in around + diagonals:
        pl.when(there)(functools.partial(signal, barrier, target))
        beside = beside + there.astype(jnp.int32)
    for t in range(1, n_cond):
        signal(barrier, ((ci + t) % n_cond, xi, yi))

    scalar_loads = [
        pltpu.make_async_copy(flux_hbm, flux, scalar_sems.at[0]),
        pltpu.make_async_copy(weights_hbm, weights, scalar_sems.at[1]),
    ]
    adjoint_loads = [
        pltpu.make_async_copy(adjoint.at[0, :, x], first.at[pl.ds(0, nvar), x], adjoint_sems.at[x])
        for x in range(nx)
    ]
    adjoint_loads.append(pltpu.make_async_copy(diagonal_hbm, first.at[nvar], adjoint_sems.at[nx]))

    source_loads = [
        pltpu.make_async_copy(source_hbm.at[0, :, x], source.at[:, x], plane_sems.at[x])
        for x in range(nx)
    ]

    late_loads = [
        pltpu.make_async_copy(src, dst, local_sems.at[i])
        for i, (src, dst) in enumerate(
            (
                (sensitivity_hbm.at[0], sensitivity),
                (mask_hbm, mask),
                (slots_hbm, slots),
                (basis_hbm, basis),
            )
        )
    ]
    for copy in scalar_loads + adjoint_loads + source_loads + late_loads:
        copy.start()

    def field(stage):
        return smoothed_out.at[0] if stage == 2 else (first, second)[stage]

    def clear_face(side):
        for stage in range(3):
            face_halo[stage, side] = jnp.zeros((nvar + 1, ny, nz), jnp.float32)
        face_halo[0, side, nvar] = jnp.ones((ny, nz), jnp.float32)

    def clear_row(side):
        for stage in range(3):
            row_halo[stage, side] = jnp.zeros((nvar + 1, nx, nz), jnp.float32)
        row_halo[0, side, nvar] = jnp.ones((nx, nz), jnp.float32)

    def clear_corner(i):
        corner[:, i : i + 1, :] = jnp.zeros((nvar, 1, nz), jnp.float32)

    corner[:, 4:, :] = jnp.zeros((nvar, 4, nz), jnp.float32)
    for i, (there, _) in enumerate(diagonals):
        pl.when(jnp.logical_not(there))(functools.partial(clear_corner, i))
    pl.when(xi == 0)(functools.partial(clear_face, 0))
    pl.when(xi == n_gx - 1)(functools.partial(clear_face, 1))
    pl.when(yi == 0)(functools.partial(clear_row, 0))
    pl.when(yi == n_yz - 1)(functools.partial(clear_row, 1))
    depth = parts.shape[1]
    if depth > 3 * block:
        for x in range(nx):
            parts[x, 3 * block :] = jnp.zeros((depth - 3 * block, nz), jnp.bfloat16)

    def remote(src, dst, sems, target):
        return pltpu.make_async_remote_copy(
            src_ref=src,
            dst_ref=dst,
            send_sem=sems[0],
            recv_sem=sems[1],
            device_id=target,
            device_id_type=MESH,
        )

    def copies(stage):
        sent = pl.ds(0, nvar + 1 if stage == 0 else nvar)

        def face(side, x):
            return face_sent.at[side] if stage == 1 else field(stage).at[:, x]

        def sems(ref, way):
            return ref.at[stage, 0, way], ref.at[stage, 1, way]

        def into(ref, side):
            return ref.at[stage, side, sent]

        up_x = remote(face(1, nx - 1), into(face_halo, 0), sems(face_sems, 0), after_x)
        down_x = remote(face(0, 0), into(face_halo, 1), sems(face_sems, 1), before_x)
        up_y = remote(edges.at[stage, 1, sent], into(row_halo, 0), sems(row_sems, 0), after_y)
        down_y = remote(edges.at[stage, 0, sent], into(row_halo, 1), sems(row_sems, 1), before_y)
        return (
            [(has_after_x, has_before_x, up_x), (has_before_x, has_after_x, down_x)],
            [(has_after_y, has_before_y, up_y), (has_before_y, has_after_y, down_y)],
        )

    corner_copies = []
    for i, (there, target) in enumerate(diagonals):
        x, side = (0, nx - 1)[i // 2], i % 2
        copy = remote(
            edges.at[0, side, pl.ds(0, nvar), pl.ds(x, 1), :],
            corner.at[:, pl.ds(3 - i, 1), :],
            (corner_sems.at[0, i], corner_sems.at[1, i]),
            target,
        )
        corner_copies.append((there, diagonals[3 - i][0], copy))

    def begin(plans):
        for go, _, copy in plans:
            pl.when(go)(copy.start)

    def receive(plans):
        for _, come, copy in plans:
            pl.when(come)(copy.wait_recv)

    def drain(plans):
        for go, _, copy in plans:
            pl.when(go)(copy.wait_send)

    def line_round(distances):
        targets = []
        for axis, distance in distances:
            here, count = (xi, n_gx) if axis == "gx" else (yi, n_yz)
            for sign in (1, -1):
                there = here + sign * distance
                target = (ci, there, yi) if axis == "gx" else (ci, xi, there)
                targets.append((jnp.logical_and(there >= 0, there < count), target))
        return targets

    gx_spans, yz_spans = spans_of(n_gx), spans_of(n_yz)
    rounds = []
    for i in range(max(len(gx_spans), len(yz_spans))):
        distances = [("gx", d) for d in gx_spans[i : i + 1]] + [("yz", d) for d in yz_spans[i : i + 1]]
        rounds.append(line_round(distances))
    always = ci >= 0
    rounds.append([(always, (ci, (xi + t) % n_gx, yi)) for t in range(1, n_gx)])
    rounds.append([(always, ((ci + t) % n_cond, xi, yi)) for t in range(1, n_cond)])

    def tell(i):
        for there, target in rounds[i]:
            pl.when(there)(functools.partial(signal, round_sems.at[i], target))

    def hear(i):
        count = 0
        for there, _ in rounds[i]:
            count = count + there.astype(jnp.int32)
        pl.semaphore_wait(round_sems.at[i], count)

    def advance(i):
        hear(i)
        if i + 1 < len(rounds):
            tell(i + 1)

    def keep_edges(kept, k, x, value):
        kept[0, k, x : x + 1, :] = value[0:1]
        kept[1, k, x : x + 1, :] = value[ny - 1 : ny]

    def rows_of(stage):
        return row_true if stage == 1 else edges.at[stage]

    def split(value):
        high = value.astype(jnp.bfloat16)
        return high, (value - high.astype(jnp.float32)).astype(jnp.bfloat16)

    column = lax.broadcasted_iota(jnp.int32, (ny, depth), 1)
    row = lax.broadcasted_iota(jnp.int32, (ny, depth), 0)
    part = column // block
    pair = column - part * block
    from_var = pair // ny
    offset = pair - from_var * ny - row

    for copy in scalar_loads:
        copy.wait()

    def spread(k, d):
        total = jnp.zeros((ny, depth), jnp.float32)
        for e in range(nvar):
            total = jnp.where(from_var == e, flux[e, k, 0, d], total)
        upper = total.astype(jnp.bfloat16).astype(jnp.float32)
        lower = (total - upper).astype(jnp.bfloat16).astype(jnp.float32)
        return jnp.where(part < 2, upper, jnp.where(part == 2, lower, 0.0))

    for k in range(nvar):
        own = jnp.where(offset == 1, spread(k, 2), jnp.where(offset == -1, spread(k, 3), 0.0))
        bands[k * ny : (k + 1) * ny, :] = own.astype(jnp.bfloat16)
        for g, d in ((1, 0), (2, 1), (3, 4), (4, 5)):
            other = jnp.where(offset == 0, spread(k, d), 0.0)
            at = g * block + k * ny
            bands[at : at + ny, :] = other.astype(jnp.bfloat16)

    pl.semaphore_wait(barrier, beside)
    tell(0)
    for copy in adjoint_loads:
        copy.wait()
    for x in range(nx):
        for k in range(nvar + 1):
            keep_edges(edges.at[0], k, x, first[k, x])
    for plans in copies(0):
        begin(plans)
    begin(corner_copies)

    dot = functools.partial(jnp.dot, preferred_element_type=jnp.float32)
    last_lane = lax.broadcasted_iota(jnp.int32, (ny, nz), 1)

    def multiply(stage, x):
        for e in range(nvar):
            high, low = split(field(stage)[e, x])
            for p, value in enumerate((high, low, high)):
                at = p * block + e * ny
                parts[x, at : at + ny, :] = value
        products[x] = dot(bands[...], parts[x])

    def gathered(x, k):
        def product(plane, g):
            at = g * block + k * ny
            return products[plane, at : at + ny, :]

        acc = source[k, x] + product(x, 0)
        if x + 1 < nx:
            acc = acc + product(x + 1, 1)
        if x > 0:
            acc = acc + product(x - 1, 2)
        up = pltpu.roll(product(x, 3), nz - 1, 1)
        down = pltpu.roll(product(x, 4), 1, 1)
        up = jnp.where(last_lane == nz - 1, 0.0, up)
        down = jnp.where(last_lane == 0, 0.0, down)
        return acc + up + down

    def relax(stage, x):
        if stage == 0:
            step = RELAX / first[nvar, x]
            step_of[x] = step
            step_edge[0, x : x + 1, :] = step[0:1]
            step_edge[1, x : x + 1, :] = step[ny - 1 : ny]
        else:
            step = step_of[x]
            cover = mask[x].astype(jnp.float32)
        total = None
        for k in range(nvar):
            value = (1.0 - RELAX) * field(stage)[k, x] + step * gathered(x, k)
            field(stage + 1)[k, x] = value
            keep_edges(edges.at[stage + 1], k, x, value)
            if stage == 0:
                keep_edges(row_true, k, x, value)
                for side, plane in ((0, 0), (1, nx - 1)):
                    if x == plane:
                        face_sent[side, k] = value
            if stage == 1:
                weight = sensitivity[k, x].astype(jnp.float32) * cover
                weight_edge[0, k, x : x + 1, :] = weight[0:1]
                weight_edge[1, k, x : x + 1, :] = weight[ny - 1 : ny]
                term = value * weight
                total = term if k == 0 else total + term
        if stage == 1:
            surface[x] = total

    def settle(stage, x):
        for k in range(nvar):
            value = gathered(x, k) - first[nvar, x] * field(2)[k, x]
            residual_out[0, k, x] = value
            keep_edges(edges.at[3], k, x, value)

    def sweep(stage, finish, between=None):
        multiply(stage, 0)
        for x in range(nx):
            if between is not None and x == nx // 2:
                between()
            if x + 1 < nx:
                multiply(stage, x + 1)
            finish(stage, x)

    def brought(cells, d):
        out = []
        for k in range(nvar):
            total = flux[0, k, 0, d] * cells[0]
            for e in range(1, nvar):
                total = total + flux[e, k, 0, d] * cells[e]
            out.append(total)
        return out

    def halo_of(halo, more, stage, side):
        cells = [halo[stage, side, e] for e in range(nvar)]
        return [c + more[side, e] for e, c in enumerate(cells)] if stage == 1 else cells

    def add_own():
        spot = lax.broadcasted_iota(jnp.int32, (8, nz), 0)
        lines_of = [corner[e] for e in range(nvar)]
        along_x, along_y = [], []
        for k in range(nvar):
            for out, near, ds in ((along_x, spot < 2, (1, 0)), (along_y, spot % 2 == 0, (3, 2))):
                total = None
                for e in range(nvar):
                    scale = jnp.where(near, flux[e, k, 0, ds[0]], flux[e, k, 0, ds[1]])
                    term = scale * lines_of[e]
                    total = term if e == 0 else total + term
                out.append(total)
        at_row = lax.broadcasted_iota(jnp.int32, (nx, nz), 0)
        at_face = lax.broadcasted_iota(jnp.int32, (ny, nz), 0)
        for side, d, there in ((0, 2, has_before_y), (1, 3, has_after_y)):
            step = jnp.where(there, RELAX / row_halo[0, side, nvar], 0.0)
            mine = brought([edges[0, side, e] for e in range(nvar)], d)
            for k in range(nvar):
                ends = along_x[k][side : side + 1], along_x[k][2 + side : 3 + side]
                extra = jnp.where(at_row == 0, ends[0], jnp.where(at_row == nx - 1, ends[1], 0.0))
                row_more[side, k] = step * (mine[k] + extra)
        for side, x, d, there in ((0, 0, 0, has_before_x), (1, nx - 1, 1, has_after_x)):
            step = jnp.where(there, RELAX / face_halo[0, side, nvar], 0.0)
            mine = brought([first[e, x] for e in range(nvar)], d)
            for k in range(nvar):
                i = 2 * side
                ends = along_y[k][i : i + 1], along_y[k][i + 1 : i + 2]
                extra = jnp.where(at_face == 0, ends[0], jnp.where(at_face == ny - 1, ends[1], 0.0))
                face_more[side, k] = step * (mine[k] + extra)

    def add_faces(stage):
        for side, x, d in ((0, 0, 1), (1, nx - 1, 0)):
            more = brought(halo_of(face_halo, face_more, stage, side), d)
            total = None
            for k in range(nvar):
                if stage == 2:
                    value = residual_out[0, k, x] + more[k]
                    residual_out[0, k, x] = value
                else:
                    part = step_of[x] * more[k]
                    value = field(stage + 1)[k, x] + part
                    field(stage + 1)[k, x] = value
                    if stage == 1:
                        term = part * sensitivity[k, x].astype(jnp.float32)
                        total = term if k == 0 else total + term
                keep_edges(rows_of(stage + 1), k, x, value)
            if stage == 1:
                surface[x] = surface[x] + total * mask[x].astype(jnp.float32)

    def add_rows(stage):
        for side, y, d in ((0, 0, 3), (1, ny - 1, 2)):
            more = brought(halo_of(row_halo, row_more, stage, side), d)
            total = None
            for k in range(nvar):
                part = more[k] if stage == 2 else step_edge[side] * more[k]
                value = rows_of(stage + 1)[side, k] + part
                if stage == 1:
                    edges[2, side, k] = value
                if stage == 1:
                    term = part * weight_edge[side, k]
                    total = term if k == 0 else total + term
                for x in range(nx):
                    if stage == 2:
                        residual_out[0, k, x, y : y + 1, :] = value[x : x + 1]
                    else:
                        field(stage + 1)[k, x, y : y + 1, :] = value[x : x + 1]
            if stage == 1:
                for x in range(nx):
                    surface[x, y : y + 1, :] = surface[x, y : y + 1, :] + total[x : x + 1]

    def complete(stage):
        faces, ranks = copies(stage)
        receive(faces)
        add_faces(stage)
        receive(ranks)
        add_rows(stage)

    for copy in source_loads:
        copy.wait()
    advance(0)
    sweep(0, relax)
    for plans in copies(1):
        begin(plans)
    for i in range(1, len(rounds) - 2):
        advance(i)
    complete(0)
    for copy in late_loads:
        copy.wait()
    sweep(1, relax, functools.partial(advance, len(rounds) - 2))
    receive(corner_copies)
    add_own()

    line = lax.broadcasted_iota(jnp.int32, (lines, nx * ny), 0)
    spots = jnp.concatenate([slots[x : x + 1, :] for x in range(nx)], axis=1)
    wanted = jnp.concatenate([2 * line, 2 * line + 1, 2 * line - 1], axis=0)
    onehot[...] = (wanted == spots).astype(jnp.float32).astype(jnp.bfloat16)
    weight_sum = weights[0]
    for c in range(1, n_cond):
        weight_sum = weight_sum + weights[c]
    share = jnp.full((1, LANES), weights[ci], jnp.int32).astype(jnp.float32) / jnp.full(
        (1, LANES), weight_sum, jnp.int32
    ).astype(jnp.float32)

    complete(1)
    for plans in copies(2):
        begin(plans)

    basis_high, basis_low = split(basis[...])
    surface_high, surface_low = split(surface[...].reshape(nx * ny, nz))
    projected = (
        dot(surface_high, basis_high) + dot(surface_high, basis_low) + dot(surface_low, basis_high)
    )
    high, low = split(projected)
    looked = dot(onehot[...], high) + dot(onehot[...], low)
    turned = pltpu.roll(looked[lines:], LANES // 2, 1)
    spot = lax.broadcasted_iota(jnp.int32, (lines, LANES), 1)
    gradient = looked[:lines] + jnp.where(spot < LANES // 2, turned[lines:], turned[:lines])
    gradient = gradient * share
    for g in range(lines // rows):
        pieces[g] = gradient[g * rows : (g + 1) * rows]

    def group(gx, yz):
        return (gx * n_yz + yz) * per_owner // (rows * LANES)

    def give(c, gx, yz):
        remote(
            pieces.at[group(gx, yz)],
            arrived.at[me],
            (piece_sems.at[0], piece_sems.at[1]),
            (c, gx, yz),
        ).start()

    arrived[me] = pieces[group(xi, yi)]
    advance(len(rounds) - 1)
    if devices <= 64:
        for dy in range(n_yz):
            for dx in range(n_gx):
                for dc in range(n_cond):
                    if dc or dx or dy:
                        give((ci + dc) % n_cond, (xi + dx) % n_gx, (yi + dy) % n_yz)
    else:

        def give_next(t, carry):
            flat = (me + t) % devices
            give(flat // (n_gx * n_yz), (flat // n_yz) % n_gx, flat % n_yz)
            return carry

        lax.fori_loop(1, devices, give_next, 0)

    sweep(2, settle)
    others = arrived.at[pl.ds(0, devices - 1)]
    for i in range(2):
        pltpu.make_async_copy(others, others, piece_sems.at[i]).wait()
    gradient_out[...] = jnp.sum(arrived[...], axis=0)
    complete(2)
    for stage in range(3):
        for plans in copies(stage):
            drain(plans)
    drain(corner_copies)


def write(smoothed, residual, gradient, smoothed_hbm, residual_hbm, gradient_hbm, sems):
    stores = [
        pltpu.make_async_copy(src, dst, sems.at[i])
        for i, (src, dst) in enumerate(
            ((smoothed, smoothed_hbm), (residual, residual_hbm), (gradient, gradient_hbm))
        )
    ]
    for copy in stores:
        copy.start()
    for copy in stores:
        copy.wait()


def local(
    adjoint,
    objective_gradient,
    diagonal,
    flux_blocks,
    flux_sensitivity,
    surface_mask,
    patch_band_slot,
    design_basis,
    condition_weights,
):
    sizes = tuple(lax.axis_size(axis) for axis in ("cond", "gx", "yz"))
    devices = sizes[0] * sizes[1] * sizes[2]
    _, nvar, nx, ny, nz = adjoint.shape
    per_owner = NDES // (sizes[1] * sizes[2])
    rows = max(1, per_owner // LANES)
    lines = NDES // LANES
    rounds = max(len(spans_of(sizes[1])), len(spans_of(sizes[2]))) + 2
    f32 = jnp.float32
    hbm = pl.BlockSpec(memory_space=pltpu.MemorySpace.HBM)
    vmem = pl.BlockSpec(memory_space=pltpu.MemorySpace.VMEM)
    depth = -(-3 * nvar * ny // (2 * LANES)) * 2 * LANES
    grant = 67043328 - 2**16 - 2 * adjoint.size * 4
    smoothed, residual, gradient = pl.pallas_call(
        functools.partial(kernel, sizes),
        out_shape=(
            pltpu.VMEM(adjoint.shape, f32),
            pltpu.VMEM(adjoint.shape, f32),
            pltpu.VMEM((rows, LANES), f32),
        ),
        in_specs=[hbm] * 9,
        out_specs=(vmem, vmem, vmem),
        scratch_shapes=[
            pltpu.VMEM((nvar + 1, nx, ny, nz), f32),
            pltpu.VMEM((nvar, nx, ny, nz), f32),
            pltpu.VMEM((nvar, nx, ny, nz), f32),
            pltpu.VMEM((nx, ny, nz), f32),
            pltpu.VMEM((5 * nvar * ny, depth), jnp.bfloat16),
            pltpu.VMEM((nx, depth, nz), jnp.bfloat16),
            pltpu.VMEM((nx, 5 * nvar * ny, nz), f32),
            pltpu.SMEM((nvar, nvar, 1, 6), f32),
            pltpu.VMEM((nvar, nx, ny, nz), jnp.bfloat16),
            pltpu.VMEM((nx, ny, nz), jnp.int32),
            pltpu.VMEM((nx, ny), jnp.int32),
            pltpu.VMEM(design_basis.shape, f32),
            pltpu.SMEM(condition_weights.shape, jnp.int32),
            pltpu.VMEM((nx, ny, nz), f32),
            pltpu.VMEM((4, 2, nvar + 1, nx, nz), f32),
            pltpu.VMEM((2, nvar, nx, nz), f32),
            pltpu.VMEM((2, nvar, ny, nz), f32),
            pltpu.VMEM((3, 2, nvar + 1, nx, nz), f32),
            pltpu.VMEM((3, 2, nvar + 1, ny, nz), f32),
            pltpu.VMEM((nvar, 8, nz), f32),
            pltpu.VMEM((2, nvar, nx, nz), f32),
            pltpu.VMEM((2, nvar, ny, nz), f32),
            pltpu.VMEM((2, nx, nz), f32),
            pltpu.VMEM((2, nvar, nx, nz), f32),
            pltpu.VMEM((3 * lines, nx * ny), jnp.bfloat16),
            pltpu.VMEM((NDES // (rows * LANES), rows, LANES), f32),
            pltpu.VMEM((devices, rows, LANES), f32),
            pltpu.SemaphoreType.DMA((2,)),
            pltpu.SemaphoreType.DMA((4,)),
            pltpu.SemaphoreType.DMA((nx + 1,)),
            pltpu.SemaphoreType.DMA((nx,)),
            pltpu.SemaphoreType.DMA((3, 2, 2)),
            pltpu.SemaphoreType.DMA((3, 2, 2)),
            pltpu.SemaphoreType.DMA((2, 4)),
            pltpu.SemaphoreType.DMA((2,)),
            pltpu.SemaphoreType.REGULAR((rounds,)),
        ],
        compiler_params=pltpu.CompilerParams(
            collective_id=0, has_side_effects=True, vmem_limit_bytes=grant
        ),
    )(
        adjoint,
        objective_gradient,
        diagonal,
        jnp.transpose(flux_blocks, (2, 3, 0, 1)),
        flux_sensitivity,
        surface_mask,
        patch_band_slot,
        design_basis,
        condition_weights,
    )
    smoothed, residual, gradient = pl.pallas_call(
        write,
        out_shape=(
            jax.ShapeDtypeStruct(adjoint.shape, f32),
            jax.ShapeDtypeStruct(adjoint.shape, f32),
            jax.ShapeDtypeStruct((rows, LANES), f32),
        ),
        in_specs=[vmem] * 3,
        out_specs=(hbm, hbm, hbm),
        scratch_shapes=[pltpu.SemaphoreType.DMA((3,))],
        compiler_params=pltpu.CompilerParams(vmem_limit_bytes=2**20),
    )(smoothed, residual, gradient)
    flat = gradient.reshape(-1)
    if per_owner < flat.shape[0]:
        owner = lax.axis_index(("gx", "yz"))
        flat = lax.dynamic_slice_in_dim(flat, (owner * per_owner) % flat.shape[0], per_owner, 0)
    return smoothed, residual, flat


def solution(mesh):
    placed = (
        P("cond", None, "gx", "yz", None),
        P("cond", None, "gx", "yz", None),
        P("gx", "yz", None),
        P("cond", None, None, None),
        P("cond", None, "gx", "yz", None),
        P("gx", "yz", None),
        P("gx", "yz"),
        P(),
        P(),
    )
    return jax.shard_map(
        local,
        mesh=mesh,
        in_specs=placed,
        out_specs=(
            P("cond", None, "gx", "yz", None),
            P("cond", None, "gx", "yz", None),
            P(("gx", "yz")),
        ),
        check_vma=False,
    )
```

time: 19.4 us -> 18.1 us (0.933)
  Pallas kernels: 18.6 us -> 17.3 us
    pallas_call x1, Pallas kernels: 17.5 us -> 16.3 us  [local(): pl.pallas_call(functools.partial(kernel, sizes), out_shape=(pltpu.VMEM(ad...]
where the time goes in v3:
time: 18.1 us; the launch traced here: 18 us
  Pallas kernels  17.3 us (96%)
  between operations  0.64 us (4%)
    pallas_call x1, Pallas kernels, local(): pl.pallas_call(functools.partial(kernel, sizes), out_shape=(pltpu.VMEM(ad...  16.3 us
    pallas_call x1, Pallas kernels, local(): pl.pallas_call(write, out_shape=(jax.ShapeDtypeStruct(adjoint.shape, f32)...  1.08 us

profile of v3, /device:TPU:0, one launch (start us, length us, event | category | flops | bytes accessed | tf_op | source)
XLA Modules:
  0.0 18.0 jit_solution(6195170540042398312)
XLA Ops:
  0.6 16.3 %shard_map.112 = (f32[1,5,8,16,256]{4,3,2,1,0:T(8,128)S(1)}, f32[1,5,8,16,256]{4,3,2,1,0:T(8,128)S(1)}, f32[2,128]{1,0:T(2,128)S(1)}) custom-call(f32[1,5,8,16,256]{4,3,2,1,0:T(8,128)} %adjoint.1, f32[1,5,8,16,256]{4,3,2,1,0:T(8,128)} %source_hbm.1, f32[8,16,256]{2,1,0:T(8,128)} %diagonal_hbm.1, f32[5,5,1,6]{3,2,1,0:T(1,128)} %bitcast.2, ...), custom_call_target="tpu_custom_call" | custom-call | tf_op jit(solution)/shard_map/pallas_call | solution.py:584
  16.9 1.1 %shard_map.113 = (f32[1,5,8,16,256]{4,3,2,1,0:T(8,128)}, f32[1,5,8,16,256]{4,3,2,1,0:T(8,128)}, f32[2,128]{1,0:T(2,128)}) custom-call(f32[1,5,8,16,256]{4,3,2,1,0:T(8,128)S(1)} %get-tuple-element.9.smoothed, f32[1,5,8,16,256]{4,3,2,1,0:T(8,128)S(1)} %get-tuple-element.10.residual, f32[2,128]{1,0:T(2,128)S(1)} %get-tuple-element.11.gradient), custom_call_target="tpu_custom_call" | custom-call | tf_op jit(solution)/shard_map/pallas_call | solution.py:645

commit v4 on v3

--- a/solution.py
+++ b/solution.py
@@ -59,17 +59,19 @@
     row_more,
     face_more,
     step_edge,
+    weight,
     weight_edge,
+    basis_parts,
     onehot,
     pieces,
     arrived,
     scalar_sems,
     local_sems,
-    adjoint_sems,
-    plane_sems,
+    early_sems,
     row_sems,
     face_sems,
     corner_sems,
+    diagonal_sems,
     piece_sems,
     round_sems,
 ):
@@ -113,15 +115,10 @@
         pltpu.make_async_copy(weights_hbm, weights, scalar_sems.at[1]),
     ]
     adjoint_loads = [
-        pltpu.make_async_copy(adjoint.at[0, :, x], first.at[pl.ds(0, nvar), x], adjoint_sems.at[x])
-        for x in range(nx)
+        pltpu.make_async_copy(adjoint.at[0], first.at[pl.ds(0, nvar)], early_sems.at[0]),
+        pltpu.make_async_copy(diagonal_hbm, first.at[nvar], early_sems.at[1]),
     ]
-    adjoint_loads.append(pltpu.make_async_copy(diagonal_hbm, first.at[nvar], adjoint_sems.at[nx]))
-
-    source_loads = [
-        pltpu.make_async_copy(source_hbm.at[0, :, x], source.at[:, x], plane_sems.at[x])
-        for x in range(nx)
-    ]
+    source_loads = [pltpu.make_async_copy(source_hbm.at[0], source, early_sems.at[2])]
 
     late_loads = [
         pltpu.make_async_copy(src, dst, local_sems.at[i])
@@ -176,10 +173,10 @@
         )
 
     def copies(stage):
-        sent = pl.ds(0, nvar + 1 if stage == 0 else nvar)
+        sent = pl.ds(0, nvar)
 
         def face(side, x):
-            return face_sent.at[side] if stage == 1 else field(stage).at[:, x]
+            return face_sent.at[side] if stage == 1 else field(stage).at[sent, x]
 
         def sems(ref, way):
             return ref.at[stage, 0, way], ref.at[stage, 1, way]
@@ -195,6 +192,21 @@
             [(has_after_x, has_before_x, up_x), (has_before_x, has_after_x, down_x)],
             [(has_after_y, has_before_y, up_y), (has_before_y, has_after_y, down_y)],
         )
+
+    def diagonal_copies():
+        def sems(way):
+            return diagonal_sems.at[0, way], diagonal_sems.at[1, way]
+
+        up_x = remote(first.at[nvar, nx - 1], face_halo.at[0, 0, nvar], sems(0), after_x)
+        down_x = remote(first.at[nvar, 0], face_halo.at[0, 1, nvar], sems(1), before_x)
+        up_y = remote(edges.at[0, 1, nvar], row_halo.at[0, 0, nvar], sems(2), after_y)
+        down_y = remote(edges.at[0, 0, nvar], row_halo.at[0, 1, nvar], sems(3), before_y)
+        return [
+            (has_after_x, has_before_x, up_x),
+            (has_before_x, has_after_x, down_x),
+            (has_after_y, has_before_y, up_y),
+            (has_before_y, has_after_y, down_y),
+        ]
 
     corner_copies = []
     for i, (there, target) in enumerate(diagonals):
@@ -300,9 +312,11 @@
     for plans in copies(0):
         begin(plans)
     begin(corner_copies)
+    begin(diagonal_copies())
 
     dot = functools.partial(jnp.dot, preferred_element_type=jnp.float32)
-    last_lane = lax.broadcasted_iota(jnp.int32, (ny, nz), 1)
+    lane = lax.broadcasted_iota(jnp.int32, (ny, LANES), 1)
+    spans = [slice(h * LANES, (h + 1) * LANES) for h in range(nz // LANES)]
 
     def multiply(stage, x):
         for e in range(nvar):
@@ -322,11 +336,14 @@
             acc = acc + product(x + 1, 1)
         if x > 0:
             acc = acc + product(x - 1, 2)
-        up = pltpu.roll(product(x, 3), nz - 1, 1)
-        down = pltpu.roll(product(x, 4), 1, 1)
-        up = jnp.where(last_lane == nz - 1, 0.0, up)
-        down = jnp.where(last_lane == 0, 0.0, down)
-        return acc + up + down
+        ahead = [pltpu.roll(product(x, 3)[:, c], LANES - 1, 1) for c in spans] + [0.0]
+        behind = [0.0] + [pltpu.roll(product(x, 4)[:, c], 1, 1) for c in spans]
+        shifted = [
+            jnp.where(lane == LANES - 1, ahead[h + 1], ahead[h])
+            + jnp.where(lane == 0, behind[h], behind[h + 1])
+            for h in range(len(spans))
+        ]
+        return acc + jnp.concatenate(shifted, axis=1)
 
     def relax(stage, x):
         if stage == 0:
@@ -336,7 +353,6 @@
             step_edge[1, x : x + 1, :] = step[ny - 1 : ny]
         else:
             step = step_of[x]
-            cover = mask[x].astype(jnp.float32)
         total = None
         for k in range(nvar):
             value = (1.0 - RELAX) * field(stage)[k, x] + step * gathered(x, k)
@@ -348,10 +364,7 @@
                     if x == plane:
                         face_sent[side, k] = value
             if stage == 1:
-                weight = sensitivity[k, x].astype(jnp.float32) * cover
-                weight_edge[0, k, x : x + 1, :] = weight[0:1]
-                weight_edge[1, k, x : x + 1, :] = weight[ny - 1 : ny]
-                term = value * weight
+                term = value * weight[k, x]
                 total = term if k == 0 else total + term
         if stage == 1:
             surface[x] = total
@@ -362,11 +375,9 @@
             residual_out[0, k, x] = value
             keep_edges(edges.at[3], k, x, value)
 
-    def sweep(stage, finish, between=None):
+    def sweep(stage, finish):
         multiply(stage, 0)
         for x in range(nx):
-            if between is not None and x == nx // 2:
-                between()
             if x + 1 < nx:
                 multiply(stage, x + 1)
             finish(stage, x)
@@ -384,35 +395,47 @@
         cells = [halo[stage, side, e] for e in range(nvar)]
         return [c + more[side, e] for e, c in enumerate(cells)] if stage == 1 else cells
 
-    def add_own():
+    def begin_own():
+        for side, d in ((0, 2), (1, 3)):
+            mine = brought([edges[0, side, e] for e in range(nvar)], d)
+            for k in range(nvar):
+                row_more[side, k] = mine[k]
+        for side, x, d in ((0, 0, 0), (1, nx - 1, 1)):
+            mine = brought([first[e, x] for e in range(nvar)], d)
+            for k in range(nvar):
+                face_more[side, k] = mine[k]
+
+    def add_corners():
         spot = lax.broadcasted_iota(jnp.int32, (8, nz), 0)
         lines_of = [corner[e] for e in range(nvar)]
-        along_x, along_y = [], []
+        at_row = lax.broadcasted_iota(jnp.int32, (nx, nz), 0)
+        at_face = lax.broadcasted_iota(jnp.int32, (ny, nz), 0)
         for k in range(nvar):
-            for out, near, ds in ((along_x, spot < 2, (1, 0)), (along_y, spot % 2 == 0, (3, 2))):
+            along = []
+            for near, ds in ((spot < 2, (1, 0)), (spot % 2 == 0, (3, 2))):
                 total = None
                 for e in range(nvar):
                     scale = jnp.where(near, flux[e, k, 0, ds[0]], flux[e, k, 0, ds[1]])
                     term = scale * lines_of[e]
                     total = term if e == 0 else total + term
-                out.append(total)
-        at_row = lax.broadcasted_iota(jnp.int32, (nx, nz), 0)
-        at_face = lax.broadcasted_iota(jnp.int32, (ny, nz), 0)
-        for side, d, there in ((0, 2, has_before_y), (1, 3, has_after_y)):
+                along.append(total)
+            for side in range(2):
+                ends = along[0][side : side + 1], along[0][2 + side : 3 + side]
+                extra = jnp.where(at_row == 0, ends[0], jnp.where(at_row == nx - 1, ends[1], 0.0))
+                row_more[side, k] = row_more[side, k] + extra
+                ends = along[1][2 * side : 2 * side + 1], along[1][2 * side + 1 : 2 * side + 2]
+                extra = jnp.where(at_face == 0, ends[0], jnp.where(at_face == ny - 1, ends[1], 0.0))
+                face_more[side, k] = face_more[side, k] + extra
+
+    def scale_more():
+        for side, there in ((0, has_before_y), (1, has_after_y)):
             step = jnp.where(there, RELAX / row_halo[0, side, nvar], 0.0)
-            mine = brought([edges[0, side, e] for e in range(nvar)], d)
             for k in range(nvar):
-                ends = along_x[k][side : side + 1], along_x[k][2 + side : 3 + side]
-                extra = jnp.where(at_row == 0, ends[0], jnp.where(at_row == nx - 1, ends[1], 0.0))
-                row_more[side, k] = step * (mine[k] + extra)
-        for side, x, d, there in ((0, 0, 0, has_before_x), (1, nx - 1, 1, has_after_x)):
+                row_more[side, k] = step * row_more[side, k]
+        for side, there in ((0, has_before_x), (1, has_after_x)):
             step = jnp.where(there, RELAX / face_halo[0, side, nvar], 0.0)
-            mine = brought([first[e, x] for e in range(nvar)], d)
             for k in range(nvar):
-                i = 2 * side
-                ends = along_y[k][i : i + 1], along_y[k][i + 1 : i + 2]
-                extra = jnp.where(at_face == 0, ends[0], jnp.where(at_face == ny - 1, ends[1], 0.0))
-                face_more[side, k] = step * (mine[k] + extra)
+                face_more[side, k] = step * face_more[side, k]
 
     def add_faces(stage):
         for side, x, d in ((0, 0, 1), (1, nx - 1, 0)):
@@ -427,11 +450,18 @@
                     value = field(stage + 1)[k, x] + part
                     field(stage + 1)[k, x] = value
                     if stage == 1:
-                        term = part * sensitivity[k, x].astype(jnp.float32)
+                        term = part * weight[k, x]
                         total = term if k == 0 else total + term
                 keep_edges(rows_of(stage + 1), k, x, value)
             if stage == 1:
-                surface[x] = surface[x] + total * mask[x].astype(jnp.float32)
+                surface[x] = surface[x] + total
+
+    def put_row(stage, k, y, value):
+        for x in range(nx):
+            if stage == 2:
+                residual_out[0, k, x, y : y + 1, :] = value[x : x + 1]
+            else:
+                field(stage + 1)[k, x, y : y + 1, :] = value[x : x + 1]
 
     def add_rows(stage):
         for side, y, d in ((0, 0, 3), (1, ny - 1, 2)):
@@ -445,11 +475,8 @@
                 if stage == 1:
                     term = part * weight_edge[side, k]
                     total = term if k == 0 else total + term
-                for x in range(nx):
-                    if stage == 2:
-                        residual_out[0, k, x, y : y + 1, :] = value[x : x + 1]
-                    else:
-                        field(stage + 1)[k, x, y : y + 1, :] = value[x : x + 1]
+                if stage != 1:
+                    put_row(stage, k, y, value)
             if stage == 1:
                 for x in range(nx):
                     surface[x, y : y + 1, :] = surface[x, y : y + 1, :] + total[x : x + 1]
@@ -467,31 +494,39 @@
     sweep(0, relax)
     for plans in copies(1):
         begin(plans)
-    for i in range(1, len(rounds) - 2):
-        advance(i)
-    complete(0)
+    begin_own()
     for copy in late_loads:
         copy.wait()
-    sweep(1, relax, functools.partial(advance, len(rounds) - 2))
-    receive(corner_copies)
-    add_own()
-
+    for x in range(nx):
+        cover = mask[x].astype(jnp.float32)
+        for k in range(nvar):
+            value = sensitivity[k, x].astype(jnp.float32) * cover
+            weight[k, x] = value
+            keep_edges(weight_edge, k, x, value)
+    basis_parts[0], basis_parts[1] = split(basis[...])
     line = lax.broadcasted_iota(jnp.int32, (lines, nx * ny), 0)
     spots = jnp.concatenate([slots[x : x + 1, :] for x in range(nx)], axis=1)
     wanted = jnp.concatenate([2 * line, 2 * line + 1, 2 * line - 1], axis=0)
     onehot[...] = (wanted == spots).astype(jnp.float32).astype(jnp.bfloat16)
+    for i in range(1, len(rounds) - 2):
+        advance(i)
+    complete(0)
+    advance(len(rounds) - 2)
+    receive(corner_copies)
+    add_corners()
+    sweep(1, relax)
     weight_sum = weights[0]
     for c in range(1, n_cond):
         weight_sum = weight_sum + weights[c]
     share = jnp.full((1, LANES), weights[ci], jnp.int32).astype(jnp.float32) / jnp.full(
         (1, LANES), weight_sum, jnp.int32
     ).astype(jnp.float32)
+    receive(diagonal_copies())
+    scale_more()
 
     complete(1)
-    for plans in copies(2):
-        begin(plans)
-
-    basis_high, basis_low = split(basis[...])
+
+    basis_high, basis_low = basis_parts[0], basis_parts[1]
     surface_high, surface_low = split(surface[...].reshape(nx * ny, nz))
     projected = (
         dot(surface_high, basis_high) + dot(surface_high, basis_low) + dot(surface_low, basis_high)
@@ -519,11 +554,12 @@
     arrived[me] = pieces[group(xi, yi)]
     advance(len(rounds) - 1)
     if devices <= 64:
-        for dy in range(n_yz):
-            for dx in range(n_gx):
-                for dc in range(n_cond):
-                    if dc or dx or dy:
-                        give((ci + dc) % n_cond, (xi + dx) % n_gx, (yi + dy) % n_yz)
+        turns = [(dc, dx, dy) for dc in range(n_cond) for dx in range(n_gx) for dy in range(n_yz)]
+        ends = ((1, n_cond - 1), (1, n_gx - 1), (1, n_yz - 1))
+        turns.sort(key=lambda t: -sum(d in e for d, e in zip(t, ends)))
+        for dc, dx, dy in turns:
+            if dc or dx or dy:
+                give((ci + dc) % n_cond, (xi + dx) % n_gx, (yi + dy) % n_yz)
     else:
 
         def give_next(t, carry):
@@ -533,16 +569,22 @@
 
         lax.fori_loop(1, devices, give_next, 0)
 
+    for side, y in ((0, 0), (1, ny - 1)):
+        for k in range(nvar):
+            put_row(1, k, y, edges[2, side, k])
+    for plans in copies(2):
+        begin(plans)
     sweep(2, settle)
-    others = arrived.at[pl.ds(0, devices - 1)]
-    for i in range(2):
-        pltpu.make_async_copy(others, others, piece_sems.at[i]).wait()
-    gradient_out[...] = jnp.sum(arrived[...], axis=0)
     complete(2)
     for stage in range(3):
         for plans in copies(stage):
             drain(plans)
     drain(corner_copies)
+    drain(diagonal_copies())
+    others = arrived.at[pl.ds(0, devices - 1)]
+    for i in range(2):
+        pltpu.make_async_copy(others, others, piece_sems.at[i]).wait()
+    gradient_out[...] = jnp.sum(arrived[...], axis=0)
 
 
 def write(smoothed, residual, gradient, smoothed_hbm, residual_hbm, gradient_hbm, sems):
@@ -614,16 +656,18 @@
             pltpu.VMEM((2, nvar, nx, nz), f32),
             pltpu.VMEM((2, nvar, ny, nz), f32),
             pltpu.VMEM((2, nx, nz), f32),
+            pltpu.VMEM((nvar, nx, ny, nz), f32),
             pltpu.VMEM((2, nvar, nx, nz), f32),
+            pltpu.VMEM((2,) + design_basis.shape, jnp.bfloat16),
             pltpu.VMEM((3 * lines, nx * ny), jnp.bfloat16),
             pltpu.VMEM((NDES // (rows * LANES), rows, LANES), f32),
             pltpu.VMEM((devices, rows, LANES), f32),
             pltpu.SemaphoreType.DMA((2,)),
             pltpu.SemaphoreType.DMA((4,)),
-            pltpu.SemaphoreType.DMA((nx + 1,)),
-            pltpu.SemaphoreType.DMA((nx,)),
+            pltpu.SemaphoreType.DMA((3,)),
             pltpu.SemaphoreType.DMA((3, 2, 2)),
             pltpu.SemaphoreType.DMA((3, 2, 2)),
+            pltpu.SemaphoreType.DMA((2, 4)),
             pltpu.SemaphoreType.DMA((2, 4)),
             pltpu.SemaphoreType.DMA((2,)),
             pltpu.SemaphoreType.REGULAR((rounds,)),

time: 18.1 us -> 17.6 us (0.972)
  Pallas kernels: 17.3 us -> 16.9 us
    pallas_call x1, Pallas kernels: 16.3 us -> 15.8 us  [local(): pl.pallas_call(functools.partial(kernel, sizes), out_shape=(pltpu.VMEM(ad...]
where the time goes in v4:
time: 17.6 us; the launch traced here: 17.5 us
  Pallas kernels  16.9 us (96%)
  between operations  0.64 us (4%)
    pallas_call x1, Pallas kernels, local(): pl.pallas_call(functools.partial(kernel, sizes), out_shape=(pltpu.VMEM(ad...  15.8 us
    pallas_call x1, Pallas kernels, local(): pl.pallas_call(write, out_shape=(jax.ShapeDtypeStruct(adjoint.shape, f32)...  1.08 us

profile of v4, /device:TPU:0, one launch (start us, length us, event | category | flops | bytes accessed | tf_op | source)
XLA Modules:
  0.0 17.5 jit_solution(16889062749669473876)
XLA Ops:
  0.6 15.8 %shard_map.112 = (f32[1,5,8,16,256]{4,3,2,1,0:T(8,128)S(1)}, f32[1,5,8,16,256]{4,3,2,1,0:T(8,128)S(1)}, f32[2,128]{1,0:T(2,128)S(1)}) custom-call(f32[1,5,8,16,256]{4,3,2,1,0:T(8,128)} %adjoint.1, f32[1,5,8,16,256]{4,3,2,1,0:T(8,128)} %source_hbm.1, f32[8,16,256]{2,1,0:T(8,128)} %diagonal_hbm.1, f32[5,5,1,6]{3,2,1,0:T(1,128)} %bitcast.2, ...), custom_call_target="tpu_custom_call" | custom-call | tf_op jit(solution)/shard_map/pallas_call | solution.py:626
  16.4 1.1 %shard_map.113 = (f32[1,5,8,16,256]{4,3,2,1,0:T(8,128)}, f32[1,5,8,16,256]{4,3,2,1,0:T(8,128)}, f32[2,128]{1,0:T(2,128)}) custom-call(f32[1,5,8,16,256]{4,3,2,1,0:T(8,128)S(1)} %get-tuple-element.9.smoothed, f32[1,5,8,16,256]{4,3,2,1,0:T(8,128)S(1)} %get-tuple-element.10.residual, f32[2,128]{1,0:T(2,128)S(1)} %get-tuple-element.11.gradient), custom_call_target="tpu_custom_call" | custom-call | tf_op jit(solution)/shard_map/pallas_call | solution.py:689

commit v5 on v4

--- a/solution.py
+++ b/solution.py
@@ -35,7 +35,7 @@
     weights_hbm,
     smoothed_out,
     residual_out,
-    gradient_out,
+    arrived,
     first,
     second,
     source,
@@ -64,7 +64,6 @@
     basis_parts,
     onehot,
     pieces,
-    arrived,
     scalar_sems,
     local_sems,
     early_sems,
@@ -584,18 +583,19 @@
     others = arrived.at[pl.ds(0, devices - 1)]
     for i in range(2):
         pltpu.make_async_copy(others, others, piece_sems.at[i]).wait()
-    gradient_out[...] = jnp.sum(arrived[...], axis=0)
-
-
-def write(smoothed, residual, gradient, smoothed_hbm, residual_hbm, gradient_hbm, sems):
+
+
+def write(smoothed, residual, arrived, smoothed_hbm, residual_hbm, gradient_hbm, gradient, sems):
     stores = [
         pltpu.make_async_copy(src, dst, sems.at[i])
         for i, (src, dst) in enumerate(
             ((smoothed, smoothed_hbm), (residual, residual_hbm), (gradient, gradient_hbm))
         )
     ]
-    for copy in stores:
+    for copy in stores[:2]:
         copy.start()
+    gradient[...] = jnp.sum(arrived[...], axis=0)
+    stores[2].start()
     for copy in stores:
         copy.wait()
 
@@ -622,13 +622,13 @@
     hbm = pl.BlockSpec(memory_space=pltpu.MemorySpace.HBM)
     vmem = pl.BlockSpec(memory_space=pltpu.MemorySpace.VMEM)
     depth = -(-3 * nvar * ny // (2 * LANES)) * 2 * LANES
-    grant = 67043328 - 2**16 - 2 * adjoint.size * 4
-    smoothed, residual, gradient = pl.pallas_call(
+    grant = 67043328 - 2**16 - 2 * adjoint.size * 4 - 2**12 * devices
+    smoothed, residual, arrived = pl.pallas_call(
         functools.partial(kernel, sizes),
         out_shape=(
             pltpu.VMEM(adjoint.shape, f32),
             pltpu.VMEM(adjoint.shape, f32),
-            pltpu.VMEM((rows, LANES), f32),
+            pltpu.VMEM((devices, rows, LANES), f32),
         ),
         in_specs=[hbm] * 9,
         out_specs=(vmem, vmem, vmem),
@@ -661,7 +661,6 @@
             pltpu.VMEM((2,) + design_basis.shape, jnp.bfloat16),
             pltpu.VMEM((3 * lines, nx * ny), jnp.bfloat16),
             pltpu.VMEM((NDES // (rows * LANES), rows, LANES), f32),
-            pltpu.VMEM((devices, rows, LANES), f32),
             pltpu.SemaphoreType.DMA((2,)),
             pltpu.SemaphoreType.DMA((4,)),
             pltpu.SemaphoreType.DMA((3,)),
@@ -695,9 +694,9 @@
         ),
         in_specs=[vmem] * 3,
         out_specs=(hbm, hbm, hbm),
-        scratch_shapes=[pltpu.SemaphoreType.DMA((3,))],
+        scratch_shapes=[pltpu.VMEM((rows, LANES), f32), pltpu.SemaphoreType.DMA((3,))],
         compiler_params=pltpu.CompilerParams(vmem_limit_bytes=2**20),
-    )(smoothed, residual, gradient)
+    )(smoothed, residual, arrived)
     flat = gradient.reshape(-1)
     if per_owner < flat.shape[0]:
         owner = lax.axis_index(("gx", "yz"))

time: 17.6 us -> 17.6 us (level)
  no operation moved by 1% of the time
where the time goes in v5:
time: 17.6 us; the launch traced here: 17.5 us
  Pallas kernels  16.8 us (95%)
  between operations  0.64 us (4%)
    pallas_call x1, Pallas kernels, local(): pl.pallas_call(functools.partial(kernel, sizes), out_shape=(pltpu.VMEM(ad...  15.7 us
    pallas_call x1, Pallas kernels, local(): pl.pallas_call(write, out_shape=(jax.ShapeDtypeStruct(adjoint.shape, f32)...  1.08 us

profile of v5, /device:TPU:0, one launch (start us, length us, event | category | flops | bytes accessed | tf_op | source)
XLA Modules:
  0.0 17.5 jit_solution(18260831320811688017)
XLA Ops:
  0.6 15.7 %shard_map.112 = (f32[1,5,8,16,256]{4,3,2,1,0:T(8,128)S(1)}, f32[1,5,8,16,256]{4,3,2,1,0:T(8,128)S(1)}, f32[32,2,128]{2,1,0:T(2,128)S(1)}) custom-call(f32[1,5,8,16,256]{4,3,2,1,0:T(8,128)} %adjoint.1, f32[1,5,8,16,256]{4,3,2,1,0:T(8,128)} %source_hbm.1, f32[8,16,256]{2,1,0:T(8,128)} %diagonal_hbm.1, f32[5,5,1,6]{3,2,1,0:T(1,128)} %bitcast.2, ...), custom_call_target="tpu_custom_call" | custom-call | tf_op jit(solution)/shard_map/pallas_call | solution.py:626
  16.4 1.1 %shard_map.113 = (f32[1,5,8,16,256]{4,3,2,1,0:T(8,128)}, f32[1,5,8,16,256]{4,3,2,1,0:T(8,128)}, f32[2,128]{1,0:T(2,128)}) custom-call(f32[1,5,8,16,256]{4,3,2,1,0:T(8,128)S(1)} %get-tuple-element.9.smoothed, f32[1,5,8,16,256]{4,3,2,1,0:T(8,128)S(1)} %get-tuple-element.10.residual, f32[32,2,128]{2,1,0:T(2,128)S(1)} %get-tuple-element.11.arrived), custom_call_target="tpu_custom_call" | custom-call | tf_op jit(solution)/shard_map/pallas_call | solution.py:688

commit v6 on v5

--- a/solution.py
+++ b/solution.py
@@ -130,7 +130,7 @@
             )
         )
     ]
-    for copy in scalar_loads + adjoint_loads + source_loads + late_loads:
+    for copy in scalar_loads + adjoint_loads + source_loads:
         copy.start()
 
     def field(stage):
@@ -312,6 +312,8 @@
         begin(plans)
     begin(corner_copies)
     begin(diagonal_copies())
+    for copy in late_loads:
+        copy.start()
 
     dot = functools.partial(jnp.dot, preferred_element_type=jnp.float32)
     lane = lax.broadcasted_iota(jnp.int32, (ny, LANES), 1)

time: 17.6 us -> 17.6 us (level)
  no operation moved by 1% of the time
where the time goes in v6:
time: 17.6 us; the launch traced here: 17.5 us
  Pallas kernels  16.8 us (95%)
  between operations  0.64 us (4%)
    pallas_call x1, Pallas kernels, local(): pl.pallas_call(functools.partial(kernel, sizes), out_shape=(pltpu.VMEM(ad...  15.7 us
    pallas_call x1, Pallas kernels, local(): pl.pallas_call(write, out_shape=(jax.ShapeDtypeStruct(adjoint.shape, f32)...  1.08 us

profile of v6, /device:TPU:0, one launch (start us, length us, event | category | flops | bytes accessed | tf_op | source)
XLA Modules:
  0.0 17.5 jit_solution(5530733192903218834)
XLA Ops:
  0.6 15.7 %shard_map.112 = (f32[1,5,8,16,256]{4,3,2,1,0:T(8,128)S(1)}, f32[1,5,8,16,256]{4,3,2,1,0:T(8,128)S(1)}, f32[32,2,128]{2,1,0:T(2,128)S(1)}) custom-call(f32[1,5,8,16,256]{4,3,2,1,0:T(8,128)} %adjoint.1, f32[1,5,8,16,256]{4,3,2,1,0:T(8,128)} %source_hbm.1, f32[8,16,256]{2,1,0:T(8,128)} %diagonal_hbm.1, f32[5,5,1,6]{3,2,1,0:T(1,128)} %bitcast.2, ...), custom_call_target="tpu_custom_call" | custom-call | tf_op jit(solution)/shard_map/pallas_call | solution.py:628
  16.4 1.1 %shard_map.113 = (f32[1,5,8,16,256]{4,3,2,1,0:T(8,128)}, f32[1,5,8,16,256]{4,3,2,1,0:T(8,128)}, f32[2,128]{1,0:T(2,128)}) custom-call(f32[1,5,8,16,256]{4,3,2,1,0:T(8,128)S(1)} %get-tuple-element.9.smoothed, f32[1,5,8,16,256]{4,3,2,1,0:T(8,128)S(1)} %get-tuple-element.10.residual, f32[32,2,128]{2,1,0:T(2,128)S(1)} %get-tuple-element.11.arrived), custom_call_target="tpu_custom_call" | custom-call | tf_op jit(solution)/shard_map/pallas_call | solution.py:690
